TPU v7x, 256 devices: a whole 4x4x8 slice. The times are simulated.
256 devices in a mesh: gx: 16 (over y_lo, x, core), gy: 16 (over z, y_hi).
Axes of the slice: x: 4, y: 4 (y_hi: 2, y_lo: 2; y = y_hi * 2 + y_lo), z: 8, core: 2. Of those that a mesh axis runs over, the one named last changes fastest.
Arguments:
- east_class: int32 [1024, 1024], P('gx', 'gy'), may hold values from 0 to 7
- south_class: int32 [1024, 1024], P('gx', 'gy'), may hold values from 0 to 7
- cond_table: float32 [8], replicated, may hold values from 0.5 to 4
- leakage: float32 [1024, 1024], P('gx', 'gy'), may hold values from 0.1 to 1
- pad_mask: int32 [1024, 1024], P('gx', 'gy'), may hold values 0 or 1
- load_current: float32 [1024, 1024, 256], P('gx', 'gy'), may hold values from -24 to 24
Outputs:
- potential: float32 [1024, 1024, 256], P('gx', 'gy')
All inputs are finite; a program needn't handle non-finite values. No bound on the sum of `pad_mask` on one device may be relied on, other than what follows from the above.
Results may differ from a plain program's by a relative error of at most 0.00002.
Values sent between devices are 32-bit elements; how exact they have to be, the bound alone decides.
No kernel may reach another device: no remote copies, remote signals or barrier semaphores. Data moves between devices by JAX's collectives and lax.ppermute only.
A program may use at most 64 MiB of HBM per device.

v0:
```python
import jax
import jax.numpy as jnp
from jax import lax
from jax.sharding import PartitionSpec as P

ITERS = 4


PAD_GAIN = 8.0
SPECTRAL_BOUND = 0.995


def with_halo(cells, sides, width):
    for axis, dim in sides:
        count = lax.axis_size(axis)
        head = lax.slice_in_dim(cells, 0, width, axis=dim)
        tail = lax.slice_in_dim(cells, cells.shape[dim] - width, cells.shape[dim], axis=dim)
        cells = jnp.concatenate(
            [
                lax.ppermute(tail, axis, [(i, (i + 1) % count) for i in range(count)]),
                cells,
                lax.ppermute(head, axis, [((i + 1) % count, i) for i in range(count)]),
            ],
            axis=dim,
        )
    return cells


def chebyshev_weights(total_steps):
    weights = [1.0]
    for position in range(1, total_steps):
        if position == 1:
            weights.append(1.0 / (1.0 - SPECTRAL_BOUND * SPECTRAL_BOUND / 2.0))
        else:
            weights.append(1.0 / (1.0 - SPECTRAL_BOUND * SPECTRAL_BOUND * weights[-1] / 4.0))
    return weights


def lookup(classes, cond_table):
    labels = jnp.arange(cond_table.shape[0], dtype=jnp.int32)
    matches = classes[:, :, None] == labels
    return jnp.sum(jnp.where(matches, cond_table, 0.0), axis=-1)


def trimmed(array, amount):
    return array[amount : array.shape[0] - amount, amount : array.shape[1] - amount]


def jacobi(padded_field, east_cond, south_cond, diagonal, source):
    neighbours = (
        east_cond[1:-1, 1:-1, None] * padded_field[1:-1, 2:]
        + east_cond[1:-1, :-2, None] * padded_field[1:-1, :-2]
    )
    neighbours = neighbours + south_cond[1:-1, 1:-1, None] * padded_field[2:, 1:-1]
    neighbours = neighbours + south_cond[:-2, 1:-1, None] * padded_field[:-2, 1:-1]
    return source + neighbours / diagonal[:, :, None]


def body(east_class, south_class, cond_table, leakage, pad_mask, load_current):
    east_cond = lookup(east_class, cond_table)
    south_cond = lookup(south_class, cond_table)
    pads = pad_mask.astype(jnp.float32)
    extra_diag = leakage + PAD_GAIN * pads
    omegas = chebyshev_weights(ITERS)
    stacked = jnp.stack([east_cond, south_cond, extra_diag, pads])
    widened = with_halo(stacked, (("gx", 1), ("gy", 2)), ITERS + 1)
    east_wide = widened[0]
    south_wide = widened[1]
    extra_wide = widened[2]
    cycle_diag = (
        east_wide[1:-1, 1:-1]
        + east_wide[1:-1, :-2]
        + south_wide[1:-1, 1:-1]
        + south_wide[:-2, 1:-1]
        + extra_wide[1:-1, 1:-1]
    )
    pads_cycle = widened[3][1:-1, 1:-1]
    load_wide = with_halo(load_current, (("gx", 0), ("gy", 1)), ITERS)
    source_all = (PAD_GAIN * pads_cycle[:, :, None] - load_wide) / cycle_diag[:, :, None]
    field = source_all
    previous = source_all
    for iteration in range(ITERS):
        cut = iteration + 1
        jacobi_value = jacobi(
            field,
            trimmed(east_wide, cut),
            trimmed(south_wide, cut),
            trimmed(cycle_diag, cut),
            trimmed(source_all, cut),
        )
        if iteration == 0:
            updated = jacobi_value
        else:
            older = trimmed(previous, 2)
            updated = omegas[iteration] * (jacobi_value - older) + older
        previous, field = (field, updated)
    return field


def solution(mesh):
    in_specs = (
        P("gx", "gy"),
        P("gx", "gy"),
        P(),
        P("gx", "gy"),
        P("gx", "gy"),
        P("gx", "gy", None),
    )
    out_specs = P("gx", "gy", None)
    return jax.shard_map(body, mesh=mesh, in_specs=in_specs, out_specs=out_specs, check_vma=False)
```

profile of v0, /device:TPU:7, one launch (start us, length us, event | category | flops | bytes accessed | tf_op | source)
XLA Modules:
  0.0 73.4 jit_solution(18324677106366761486)
XLA Ops:
  0.0 0.8 %convert_bitcast_fusion = f32[1,64,64]{2,1,0:T(8,128)S(1)} fusion(s32[64,64]{1,0:T(8,128)} %param.10), kind=kLoop, calls=%fused_computation.65 | loop fusion | flops 4096 | bytes 32768 | tf_op jit(solution)/shard_map/stack | solution.py:65
  0.8 0.8 %add_bitcast_fusion = f32[1,64,64]{2,1,0:T(8,128)S(1)} fusion(f32[64,64]{1,0:T(8,128)} %param.9, s32[64,64]{1,0:T(8,128)} %param.10), kind=kLoop, calls=%fused_computation.64 | loop fusion | flops 12288 | bytes 49152 | tf_op jit(solution)/shard_map/stack | solution.py:65
  1.5 1.0 %select_reduce_fusion.1 = (f32[64,64]{1,0:T(8,128)S(1)}, f32[64,64]{1,0:T(8,128)S(1)}) fusion(f32[8]{0:T(128)} %param.8, s32[64,64]{1,0:T(8,128)} %param.6, s32[64,64]{1,0:T(8,128)} %param.7), kind=kLoop, calls=%fused_computation.51 | loop fusion | flops 188416 | bytes 65568 | tf_op jit(solution)/shard_map/reduce_sum | solution.py:42
  2.6 1.8 %collective-permute-start = (f32[4,5,64]{2,1,0:T(8,128)S(1)}, f32[4,5,64]{2,1,0:T(8,128)S(1)}, u32[]{:S(2)}, u32[]{:S(2)}) collective-permute-start(f32[4,5,64]{2,1,0:T(8,128)S(1)} %get-tuple-element.17), channel_id=1, source_target_pairs={{0,16},{16,32},{32,48},{48,64},{64,80},{80,96},{96,112},{112,128},... | collective-permute-start | bytes 15368 | tf_op jit(solution)/shard_map/ppermute | solution.py:20
  4.4 4.6 %copy.34 = f32[64,64,256]{2,0,1:T(8,128)S(1)} copy(f32[64,64,256]{2,1,0:T(8,128)} %param.11) | data formatting | bytes 8388608 | tf_op args[5]
  9.1 0.6 collective-permute-done.1
  9.7 0.1 fusion.29
  9.9 2.7 %collective-permute-start.2 = (f32[4,74,5]{2,1,0:T(8,128)S(1)}, f32[4,74,5]{2,1,0:T(8,128)S(1)}, u32[]{:S(2)}, u32[]{:S(2)}) collective-permute-start(f32[4,74,5]{2,1,0:T(8,128)S(1)} %get-tuple-element.15), channel_id=1, source_target_pairs={{0,1},{1,2},{2,3},{3,4},{4,5},{5,6},{6,7},{7,8},{8,9},{9,10},{10,1... | collective-permute-start | bytes 17768 | tf_op jit(solution)/shard_map/ppermute | solution.py:20
  12.6 5.4 %collective-permute-start.3 = (f32[4,74,5]{2,1,0:T(8,128)S(1)}, f32[4,74,5]{2,1,0:T(8,128)S(1)}, u32[]{:S(2)}, u32[]{:S(2)}) collective-permute-start(f32[4,74,5]{2,1,0:T(8,128)S(1)} %get-tuple-element.16), channel_id=1, source_target_pairs={{1,0},{2,1},{3,2},{4,3},{5,4},{6,5},{7,6},{8,7},{9,8},{10,9},{11,1... | collective-permute-start | bytes 17768 | tf_op jit(solution)/shard_map/ppermute | solution.py:22
  18.0 3.0 %collective-permute-start.4 = (f32[4,64,256]{2,0,1:T(4,128)S(1)}, f32[4,64,256]{2,0,1:T(4,128)S(1)}, u32[]{:S(2)}, u32[]{:S(2)}) collective-permute-start(f32[4,64,256]{2,0,1:T(4,128)S(1)} %get-tuple-element.9), channel_id=1, source_target_pairs={{0,16},{16,32},{32,48},{48,64},{64,80},{80,96},{96,112},{112,128},... | collective-permute-start | bytes 786440 | tf_op jit(solution)/shard_map/ppermute | solution.py:20
  21.0 1.1 %collective-permute-done.2 = f32[4,74,5]{2,1,0:T(8,128)S(1)} collective-permute-done((f32[4,74,5]{2,1,0:T(8,128)S(1)}, f32[4,74,5]{2,1,0:T(8,128)S(1)}, u32[]{:S(2)}, u32[]{:S(2)}) %collective-permute-start.2) | collective-permute-done | bytes 5952 | tf_op jit(solution)/shard_map/ppermute | solution.py:20
  22.1 0.6 collective-permute-done.3
  22.7 0.2 pad_maximum_fusion.4
  22.9 0.1 fusion.36
  23.0 0.1 fusion.34
  23.1 0.1 fusion.32
  23.2 1.1 %collective-permute-done.4 = f32[4,64,256]{2,0,1:T(4,128)S(1)} collective-permute-done((f32[4,64,256]{2,0,1:T(4,128)S(1)}, f32[4,64,256]{2,0,1:T(4,128)S(1)}, u32[]{:S(2)}, u32[]{:S(2)}) %collective-permute-start.4) | collective-permute-done | bytes 262176 | tf_op jit(solution)/shard_map/ppermute | solution.py:20
  24.3 4.7 %collective-permute-done.5 = f32[4,64,256]{2,0,1:T(4,128)S(1)} collective-permute-done((f32[4,64,256]{2,0,1:T(4,128)S(1)}, f32[4,64,256]{2,0,1:T(4,128)S(1)}, u32[]{:S(2)}, u32[]{:S(2)}) %collective-permute-start.5) | collective-permute-done | bytes 262176 | tf_op jit(solution)/shard_map/ppermute | solution.py:22
  29.2 5.1 %collective-permute-start.7 = (f32[72,4,256]{2,0,1:T(8,128)S(1)}, f32[72,4,256]{2,0,1:T(8,128)S(1)}, u32[]{:S(2)}, u32[]{:S(2)}) collective-permute-start(f32[72,4,256]{2,0,1:T(8,128)S(1)} %get-tuple-element.8), channel_id=1, source_target_pairs={{1,0},{2,1},{3,2},{4,3},{5,4},{6,5},{7,6},{8,7},{9,8},{10,9},{11,1... | collective-permute-start | bytes 884744 | tf_op jit(solution)/shard_map/ppermute | solution.py:22
  34.3 0.1 slice_add_fusion
  34.9 0.1 copy.45
  35.0 0.1 copy.41
  35.1 0.1 copy.42
  36.4 0.1 fusion.30
  36.9 3.8 %collective-permute-done.6 = f32[72,4,256]{2,0,1:T(8,128)S(1)} collective-permute-done((f32[72,4,256]{2,0,1:T(8,128)S(1)}, f32[72,4,256]{2,0,1:T(8,128)S(1)}, u32[]{:S(2)}, u32[]{:S(2)}) %collective-permute-start.6) | collective-permute-done | bytes 294944 | tf_op jit(solution)/shard_map/ppermute | solution.py:20
  40.7 1.5 %collective-permute-done.7 = f32[72,4,256]{2,0,1:T(8,128)S(1)} collective-permute-done((f32[72,4,256]{2,0,1:T(8,128)S(1)}, f32[72,4,256]{2,0,1:T(8,128)S(1)}, u32[]{:S(2)}, u32[]{:S(2)}) %collective-permute-start.7) | collective-permute-done | bytes 294944 | tf_op jit(solution)/shard_map/ppermute | solution.py:22
  42.2 5.3 %fusion = f32[72,72,256]{2,0,1:T(8,128)S(1)} fusion(f32[72,4,256]{2,0,1:T(8,128)S(1)} %collective-permute-done.7, f32[4,64,256]{2,0,1:T(4,128)S(1)} %collective-permute-done.5, f32[64,64,256]{2,0,1:T(8,128)} %copy-done, f32[4,64,256]{2,0,1:T(4,128)S(1)} %collective-permute-done.4, f32[72,4,256]{2,0,1:T(8,128)S(1)} %collective-permute-done.6, ...), kind=kLoop, calls=%fused_computation.2 | loop fusion | flops 7962624 | bytes 10658304 | tf_op jit(solution)/shard_map/div | solution.py:79
  47.5 4.5 %fusion.3 = f32[70,70,256]{2,0,1:T(8,128)S(1)} fusion(f32[72,72,256]{2,0,1:T(8,128)S(1)} %fusion, f32[70,70]{0,1:T(8,128)S(1)} %copy.45, f32[70,70]{0,1:T(8,128)S(1)} %copy.44, f32[70,70]{0,1:T(8,128)S(1)} %copy.43, f32[70,70]{0,1:T(8,128)S(1)} %copy.42, f32[70,70]{0,1:T(8,128)S(1)} %copy.41), kind=kLoop, calls=%fused_computation.6 | loop fusion | flops 11289600 | bytes 30203600 | tf_op jit(solution)/shard_map/add | solution.py:56
  52.1 5.0 %fusion.7 = f32[68,68,256]{2,0,1:T(8,128)S(1)} fusion(f32[70,70,256]{2,0,1:T(8,128)S(1)} %fusion.3, f32[72,72,256]{2,0,1:T(8,128)S(1)} %fusion, f32[68,68]{0,1:T(8,128)S(1)} %copy.49, f32[68,68]{0,1:T(8,128)S(1)} %copy.48, f32[68,68]{0,1:T(8,128)S(1)} %copy.47, f32[68,68]{0,1:T(8,128)S(1)} %copy.46, f32[68,68]{0,1:T(8,128)S(1)} %copy.40), kind=kLoop, calls=%fused_computation.13 | loop fusion | flops 14204928 | bytes 28502336 | tf_op jit(solution)/shard_map/add | solution.py:95
  57.1 6.4 %fusion.17 = f32[66,66,256]{2,0,1:T(8,128)S(1)} fusion(f32[68,68,256]{2,0,1:T(8,128)S(1)} %fusion.7, f32[70,70,256]{2,0,1:T(8,128)S(1)} %fusion.3, f32[72,72,256]{2,0,1:T(8,128)S(1)} %fusion, f32[66,66]{0,1:T(8,128)S(1)} %copy.53, f32[66,66]{0,1:T(8,128)S(1)} %copy.52, f32[66,66]{0,1:T(8,128)S(1)} %copy.51, f32[66,66]{0,1:T(8,128)S(1)} %copy.50, ...), kind=kLoop, calls=%fused_computation.28 | loop fusion | flops 13381632 | bytes 31310928 | tf_op jit(solution)/shard_map/add | solution.py:95
  63.5 5.4 %fusion.25 = f32[64,64,256]{2,0,1:T(8,128)S(1)} fusion(f32[66,66,256]{2,0,1:T(8,128)S(1)} %fusion.17, f32[68,68,256]{2,0,1:T(8,128)S(1)} %fusion.7, f32[72,72,256]{2,0,1:T(8,128)S(1)} %fusion, f32[64,64]{0,1:T(8,128)S(1)} %copy.57, f32[64,64]{0,1:T(8,128)S(1)} %copy.56, f32[64,64]{0,1:T(8,128)S(1)} %copy.55, f32[64,64]{0,1:T(8,128)S(1)} %copy.54, ...), kind=kLoop, calls=%fused_computation.40 | loop fusion | flops 12582912 | bytes 29442048 | tf_op jit(solution)/shard_map/add | solution.py:95
  68.9 4.4 %copy.58 = f32[64,64,256]{2,1,0:T(8,128)} copy(f32[64,64,256]{2,0,1:T(8,128)S(1)} %fusion.25) | data formatting | bytes 8388608 | tf_op jit(solution)/shard_map/add | solution.py:95
  (34 shorter events, 2.3 us)
Async XLA Ops:
  2.6 6.5 %collective-permute-start = (f32[4,5,64]{2,1,0:T(8,128)S(1)}, f32[4,5,64]{2,1,0:T(8,128)S(1)}, u32[]{:S(2)}, u32[]{:S(2)}) collective-permute-start(f32[4,5,64]{2,1,0:T(8,128)S(1)} %get-tuple-element.17), channel_id=1, source_target_pairs={{0,16},{16,32},{32,48},{48,64},{64,80},{80,96},{96,112},{112,128},... | collective-permute-start | bytes 15368 | tf_op jit(solution)/shard_map/ppermute | solution.py:20
  4.4 5.3 %collective-permute-start.1 = (f32[4,5,64]{2,1,0:T(8,128)S(1)}, f32[4,5,64]{2,1,0:T(8,128)S(1)}, u32[]{:S(2)}, u32[]{:S(2)}) collective-permute-start(f32[4,5,64]{2,1,0:T(8,128)S(1)} %get-tuple-element.18), channel_id=1, source_target_pairs={{16,0},{32,16},{48,32},{64,48},{80,64},{96,80},{112,96},{128,112},... | collective-permute-start | bytes 15368 | tf_op jit(solution)/shard_map/ppermute | solution.py:22
  9.1 20.0 %copy-start = (f32[64,64,256]{2,0,1:T(8,128)}, f32[64,64,256]{2,0,1:T(8,128)S(1)}, u32[]{:S(2)}) copy-start(f32[64,64,256]{2,0,1:T(8,128)S(1)} %copy.34) | copy-start | bytes 12582916
  9.9 12.3 %collective-permute-start.2 = (f32[4,74,5]{2,1,0:T(8,128)S(1)}, f32[4,74,5]{2,1,0:T(8,128)S(1)}, u32[]{:S(2)}, u32[]{:S(2)}) collective-permute-start(f32[4,74,5]{2,1,0:T(8,128)S(1)} %get-tuple-element.15), channel_id=1, source_target_pairs={{0,1},{1,2},{2,3},{3,4},{4,5},{5,6},{6,7},{7,8},{8,9},{9,10},{10,1... | collective-permute-start | bytes 17768 | tf_op jit(solution)/shard_map/ppermute | solution.py:20
  12.6 10.2 %collective-permute-start.3 = (f32[4,74,5]{2,1,0:T(8,128)S(1)}, f32[4,74,5]{2,1,0:T(8,128)S(1)}, u32[]{:S(2)}, u32[]{:S(2)}) collective-permute-start(f32[4,74,5]{2,1,0:T(8,128)S(1)} %get-tuple-element.16), channel_id=1, source_target_pairs={{1,0},{2,1},{3,2},{4,3},{5,4},{6,5},{7,6},{8,7},{9,8},{10,9},{11,1... | collective-permute-start | bytes 17768 | tf_op jit(solution)/shard_map/ppermute | solution.py:22
  18.0 6.3 %collective-permute-start.4 = (f32[4,64,256]{2,0,1:T(4,128)S(1)}, f32[4,64,256]{2,0,1:T(4,128)S(1)}, u32[]{:S(2)}, u32[]{:S(2)}) collective-permute-start(f32[4,64,256]{2,0,1:T(4,128)S(1)} %get-tuple-element.9), channel_id=1, source_target_pairs={{0,16},{16,32},{32,48},{48,64},{64,80},{80,96},{96,112},{112,128},... | collective-permute-start | bytes 786440 | tf_op jit(solution)/shard_map/ppermute | solution.py:20
  21.0 8.0 %collective-permute-start.5 = (f32[4,64,256]{2,0,1:T(4,128)S(1)}, f32[4,64,256]{2,0,1:T(4,128)S(1)}, u32[]{:S(2)}, u32[]{:S(2)}) collective-permute-start(f32[4,64,256]{2,0,1:T(4,128)S(1)} %get-tuple-element.10), channel_id=1, source_target_pairs={{16,0},{32,16},{48,32},{64,48},{80,64},{96,80},{112,96},{128,112},... | collective-permute-start | bytes 786440 | tf_op jit(solution)/shard_map/ppermute | solution.py:22
  29.1 11.6 %collective-permute-start.6 = (f32[72,4,256]{2,0,1:T(8,128)S(1)}, f32[72,4,256]{2,0,1:T(8,128)S(1)}, u32[]{:S(2)}, u32[]{:S(2)}) collective-permute-start(f32[72,4,256]{2,0,1:T(8,128)S(1)} %get-tuple-element.7), channel_id=1, source_target_pairs={{0,1},{1,2},{2,3},{3,4},{4,5},{5,6},{6,7},{7,8},{8,9},{9,10},{10,1... | collective-permute-start | bytes 884744 | tf_op jit(solution)/shard_map/ppermute | solution.py:20
  29.2 13.0 %collective-permute-start.7 = (f32[72,4,256]{2,0,1:T(8,128)S(1)}, f32[72,4,256]{2,0,1:T(8,128)S(1)}, u32[]{:S(2)}, u32[]{:S(2)}) collective-permute-start(f32[72,4,256]{2,0,1:T(8,128)S(1)} %get-tuple-element.8), channel_id=1, source_target_pairs={{1,0},{2,1},{3,2},{4,3},{5,4},{6,5},{7,6},{8,7},{9,8},{10,9},{11,1... | collective-permute-start | bytes 884744 | tf_op jit(solution)/shard_map/ppermute | solution.py:22
where the time goes:
time: 73.8 us; the launch traced here: 73.4 us
  other arithmetic  29.7 us (40%)
  starting transfers between devices  18.1 us (25%)
  waiting for transfers between devices  13.4 us (18%)
  local copies, waits for them, and re-layouts  12 us (16%)
    add x3, other arithmetic, body(): updated = omegas[iteration] * (jacobi_value - older) + older  16.9 us
    ppermute x4, starting transfers between devices, with_halo(): lax.ppermute(head, axis, [((i + 1) % count, i) for i in range(count)])  10.5 us
    ppermute x4, starting transfers between devices, with_halo(): lax.ppermute(tail, axis, [(i, (i + 1) % count) for i in range(count)])  7.62 us
    ppermute x4, waiting for transfers between devices, with_halo(): lax.ppermute(head, axis, [((i + 1) % count, i) for i in range(count)])  7.35 us
    ppermute x4, waiting for transfers between devices, with_halo(): lax.ppermute(tail, axis, [(i, (i + 1) % count) for i in range(count)])  6.06 us
    div x1, other arithmetic, body(): (PAD_GAIN * pads_cycle[:, :, None] - load_wide) / cycle_diag[:, :, None]  5.34 us
    unnamed x3, local copies, waits for them, and re-layouts  4.62 us
    add x1, other arithmetic, jacobi(): return source + neighbours / diagonal[:, :, None]  4.52 us
  transfers between devices with their start and end apart: 8, of which 7 were waited for; matrix products, arithmetic and copies ran while one was open for 11% of the time, Pallas kernels for 0%

commit v1 on v0

v1 whole, which is shorter than its diff:
```python
import jax
import jax.numpy as jnp
from jax import lax
from jax.experimental import pallas as pl
from jax.experimental.pallas import tpu as pltpu
from jax.sharding import PartitionSpec as P


PAD_GAIN = 8.0
SPECTRAL_BOUND = 0.995


SIDE = 64
ROWS = SIDE + 8
COLS = SIDE + 16
GX_MSG = 8 * SIDE + SIDE
GY_MSG = 8 * SIDE + 16
CORNER_MSG = 64 + 16
F32 = jnp.float32


def weights():
    b2 = SPECTRAL_BOUND * SPECTRAL_BOUND
    first = 1.0 / (1.0 - b2 / 2.0)
    second = 1.0 / (1.0 - b2 * first / 4.0)
    third = 1.0 / (1.0 - b2 * second / 4.0)
    return first, second, third


W1, W2, W3 = weights()
MIX = W3 + (1.0 - W3) * W1
TOP = W1 * W2 * W3


def lanes_of(shape):
    return lax.broadcasted_iota(jnp.int32, shape, 1)


def coefficients(te, ts, tx, k):
    east = te[k : k + 8, :]
    west = te[k - 1 : k + 7, :]
    south = ts[k : k + 8, :]
    north = pltpu.roll(south, 1, 1)
    ground = tx[k : k + 8, :]
    inverse = 1.0 / (east + west + south + north + ground)
    fixed = jnp.where(ground > 4.0, PAD_GAIN, 0.0) * inverse
    return east * inverse, west * inverse, south * inverse, north * inverse, fixed, inverse


def spread(values, lane):
    return jnp.broadcast_to(values[:, lane : lane + 1], (8, 128))


def set_factors(factors, coef, s, row, c):
    lane = row + 4
    for which in range(4):
        coef[which, row, c : c + 8, :] = spread(factors[which], lane)
    fixed, inverse = spread(factors[4], lane), spread(factors[5], lane)
    for half in range(2):
        s[half, row, c : c + 8, :] = fixed - s[half, row, c : c + 8, :] * inverse


def sweep(src, coef, first, last, columns, unroll, emit):
    for c in columns:

        def rows(base, count, c=c):
            above = [src[half, base - 1, c : c + 8, :] for half in range(2)]
            here = [src[half, base, c : c + 8, :] for half in range(2)]
            for step in range(count):
                row = base + step
                factor = [coef[which, row, c : c + 8, :] for which in range(4)]
                for half in range(2):
                    below = src[half, row + 1, c : c + 8, :]
                    total = factor[0] * src[half, row, c + 1 : c + 9, :] + factor[1] * src[half, row, c - 1 : c + 7, :]
                    total = total + (factor[2] * below + factor[3] * above[half])
                    emit(half, row, c, total, here[half])
                    above[half], here[half] = here[half], below

        full = (last - first) // unroll
        if full == 1:
            rows(first, unroll)
        elif full > 1:

            def trip(index, carry, rows=rows):
                rows(first + index * unroll, unroll)
                return carry

            lax.fori_loop(0, full, trip, 0)
        if first + full * unroll < last:
            rows(first + full * unroll, last - first - full * unroll)


def chain(s, x1, u, t, coef, store, spans, windows, unroll):
    def to_x1(half, row, c, total, here):
        x1[half, row, c : c + 8, :] = here + total

    def to_u(half, row, c, total, here):
        u[half, row, c : c + 8, :] = total

    def to_t(half, row, c, total, here):
        t[half, row, c : c + 8, :] = total

    def to_out(half, row, c, total, here):
        store(
            half,
            row,
            c,
            s[half, row, c : c + 8, :] + (MIX * u[half, row, c : c + 8, :] + TOP * total),
        )

    for src, emit, (first, last), columns in zip((s, x1, u, t), (to_x1, to_u, to_t, to_out), spans, windows):
        sweep(src, coef, first, last, columns, unroll, emit)


def pack_kernel(*refs):
    small, load = refs[:5], refs[5]
    to_right, to_left, to_down, to_up, te, ts, tx = refs[6:13]
    edge, sem_edge, sem_rows, sem_small = refs[18:]
    table, east_class, south_class, leakage, pad_mask = refs[13:18]
    edges, tops = [], []
    nodes = [pltpu.make_async_copy(source, target, sem_small.at[i]) for i, (source, target) in enumerate(zip(small, refs[13:18]))]
    for copy in nodes:
        copy.start()
    for side in range(2):
        for half in range(2):
            copy = pltpu.make_async_copy(
                load.at[:, pl.ds(side * (SIDE - 8), 8), pl.ds(half * 128, 128)], edge.at[side, half], sem_edge.at[side, half]
            )
            copy.start()
            edges.append(copy)
    for side, message in enumerate((to_up, to_down)):
        for half in range(2):
            for row in range(4):
                copy = pltpu.make_async_copy(
                    load.at[side * (SIDE - 4) + row, :, pl.ds(half * 128, 128)],
                    message.at[pl.ds((half * 4 + row) * SIDE, SIDE), :],
                    sem_rows.at[side, half, row],
                )
                copy.start()
                tops.append(copy)

    for copy in nodes:
        copy.wait()

    def look_up(classes):
        found = jnp.zeros((SIDE, SIDE), F32)
        for label in range(8):
            found = jnp.where(classes == label, table[label], found)
        return found

    zeros = jnp.zeros((SIDE, 128 - SIDE), F32)

    def turned(values):
        return pltpu.roll(jnp.concatenate([values.T, zeros], axis=1), 8, 1)

    east = turned(look_up(east_class[...]))
    south = turned(look_up(south_class[...]))
    ground = turned(leakage[...] + PAD_GAIN * pad_mask[...].astype(F32))
    for target, values in ((te, east), (ts, south), (tx, ground)):
        target[0:8, :] = jnp.zeros((8, 128), F32)
        target[8 : SIDE + 8, :] = values
        target[SIDE + 8 : SIDE + 16, :] = jnp.zeros((8, 128), F32)
    lane = lanes_of((SIDE, 128))

    def banded(shifts):
        first, second, third = [
            values if shift == 0 else pltpu.roll(values, shift, 1) for values, shift in zip((east, south, ground), shifts)
        ]
        return jnp.where(lane < 8, first, jnp.where(lane < 16, second, third))

    to_down[8 * SIDE :, :] = banded((64, 72, 80))
    to_up[8 * SIDE :, :] = banded((120, 0, 8))
    put_conductances(to_right, 8 * SIDE, te, ts, tx, SIDE + 3, SIDE + 4)
    put_conductances(to_left, 8 * SIDE, te, ts, tx, 8, 8)
    for copy in edges:
        copy.wait()
    for side, message in enumerate((to_left, to_right)):
        for half in range(2):
            for row in range(SIDE):
                base = (half * SIDE + row) * 4
                message[base : base + 4, :] = edge[side, half, row, side * 4 : side * 4 + 4, :]
    for copy in tops:
        copy.wait()


def put_conductances(message, base, te, ts, tx, first_east, first_other):
    message[base : base + 5, :] = te[first_east : first_east + 5, :]
    message[base + 5 : base + 9, :] = ts[first_other : first_other + 4, :]
    message[base + 9 : base + 13, :] = tx[first_other : first_other + 4, :]
    message[base + 13 : base + 16, :] = jnp.zeros((3, 128), F32)


def inner_kernel(te, ts, tx, load, s, x1, u, t, coef, out, done, sem_in, sem_out):
    chunk = SIDE // 4
    copies = []
    for part in range(4):
        for half in range(2):
            copy = pltpu.make_async_copy(
                load.at[pl.ds(part * chunk, chunk), :, pl.ds(half * 128, 128)],
                s.at[half, pl.ds(4 + part * chunk, chunk), pl.ds(8, SIDE), :],
                sem_in.at[part, half],
            )
            copy.start()
            copies.append(copy)
    blocks = [coefficients(te, ts, tx, 8 + 8 * block) for block in range(SIDE // 8)]
    for part in range(4):
        copies[2 * part].wait()
        copies[2 * part + 1].wait()
        for block in range(SIDE // 8):
            for row in range(part * chunk, part * chunk + chunk):
                if row:
                    set_factors(blocks[block], coef, s, row + 4, 8 + 8 * block)

    def store(half, row, c, value):
        done[half, row - 4, c - 8 : c, :] = value

    everything = range(8, SIDE + 8, 8)
    middle = range(16, SIDE, 8)
    spans = ((6, SIDE + 2), (7, SIDE + 1), (8, SIDE), (9, SIDE - 1))
    chain(s, x1, u, t, coef, store, spans, (everything, everything, everything, middle), 10)
    outs = []
    for half in range(2):
        copy = pltpu.make_async_copy(
            done.at[half, pl.ds(5, SIDE - 10), pl.ds(8, SIDE - 16), :],
            out.at[pl.ds(5, SIDE - 10), pl.ds(8, SIDE - 16), pl.ds(half * 128, 128)],
            sem_out.at[half],
        )
        copy.start()
        outs.append(copy)
    for copy in outs:
        copy.wait()


def corner_kernel(te, ts, tx, from_up, from_down, to_right, to_left, te2, ts2, tx2):
    lane = lanes_of((SIDE, 128))
    upper, lower = from_up[8 * SIDE :, :], from_down[8 * SIDE :, :]
    for source, target, down, up in ((te, te2, 0, 72), (ts, ts2, 120, 64), (tx, tx2, 112, 56)):
        head = pltpu.roll(upper, down, 1) if down else upper
        tail = pltpu.roll(lower, up, 1)
        own = source[8 : SIDE + 8, :]
        target[0:8, :] = jnp.zeros((8, 128), F32)
        target[8 : SIDE + 8, :] = jnp.where(lane < 8, head, jnp.where(lane < SIDE + 8, own, tail))
        target[SIDE + 8 : SIDE + 16, :] = jnp.zeros((8, 128), F32)
    for message, first in ((to_right, SIDE - 4), (to_left, 0)):
        for half in range(2):
            for row in range(8):
                origin = from_up if row < 4 else from_down
                base = (half * 8 + row) * 4
                at = (half * 4 + row % 4) * SIDE + first
                message[base : base + 4, :] = origin[at : at + 4, :]
    put_conductances(to_right, 64, te2, ts2, tx2, SIDE + 3, SIDE + 4)
    put_conductances(to_left, 64, te2, ts2, tx2, 8, 8)


def rows_kernel(te, ts, tx, from_up, from_down, own_up, *rest):
    s, x1, u, t, coef, out, done, sem_out = rest[6:]
    for half in range(2):
        for row in range(4):
            at = (half * 4 + row) * SIDE
            s[half, row, 8 : SIDE + 8, :] = from_up[at : at + SIDE, :]
            s[half, SIDE + 4 + row, 8 : SIDE + 8, :] = from_down[at : at + SIDE, :]
        s[half, 4, 8 : SIDE + 8, :] = own_up[half * 4 * SIDE : half * 4 * SIDE + SIDE, :]
    for block in range(SIDE // 8):
        factors = coefficients(te, ts, tx, 8 + 8 * block)
        for row in (0, 1, 2, 3, 4, SIDE + 4, SIDE + 5, SIDE + 6, SIDE + 7):
            set_factors(factors, coef, s, row, 8 + 8 * block)
    everything = range(8, SIDE + 8, 8)
    middle = range(16, SIDE, 8)
    windows = (everything, everything, everything, middle)
    outs = []
    for side, first in enumerate((1, SIDE + 2)):
        spans = tuple((first + shift, first + shift + 5) for shift in ((0, 1, 2, 3), (0, -1, -2, -3))[side])

        def store(half, row, c, value, side=side):
            done[half, row - 4 if side == 0 else row - (SIDE - 1) + 5, c - 8 : c, :] = value

        chain(s, x1, u, t, coef, store, spans, windows, 5)
        for half in range(2):
            copy = pltpu.make_async_copy(
                done.at[half, pl.ds(5 * side, 5), pl.ds(8, SIDE - 16), :],
                out.at[pl.ds(side * (SIDE - 5), 5), pl.ds(8, SIDE - 16), pl.ds(half * 128, 128)],
                sem_out.at[side, half],
            )
            copy.start()
            outs.append(copy)
    for copy in outs:
        copy.wait()


def sides_kernel(te2, ts2, tx2, from_up, from_down, own_left, from_left, from_right, corner_left, corner_right, *rest):
    s, x1, u, t, coef, out, te, ts, tx, done, sem_out = rest[6:]
    for source, target in ((te2, te), (ts2, ts), (tx2, tx)):
        target[...] = source[...]
    for main, corner, first_east, first_other in ((from_left, corner_left, 3, 4), (from_right, corner_right, SIDE + 8, SIDE + 8)):
        lane = lanes_of((16, 128))
        merged = jnp.where((lane >= 8) & (lane < SIDE + 8), main[8 * SIDE :, :], corner[64:, :])
        te[first_east : first_east + 5, :] = merged[0:5, :]
        ts[first_other : first_other + 4, :] = merged[5:9, :]
        tx[first_other : first_other + 4, :] = merged[9:13, :]
    outs = []
    for side, (main, corner, c) in enumerate(((from_left, corner_left, 1), (from_right, corner_right, SIDE + 8))):
        halo = 4 if side == 0 else SIDE + 8
        factors = coefficients(te, ts, tx, c)
        for row in range(ROWS):
            for half in range(2):
                if 4 <= row < SIDE + 4:
                    at = (half * SIDE + row - 4) * 4
                    s[half, row, halo : halo + 4, :] = main[at : at + 4, :]
                    if side == 0:
                        s[half, row, 8:9, :] = own_left[at : at + 1, :]
                else:
                    part = row if row < 4 else row - SIDE
                    at = (half * 8 + part) * 4
                    s[half, row, halo : halo + 4, :] = corner[at : at + 4, :]
                    if side == 0:
                        at = (half * 4 + part % 4) * SIDE
                        s[half, row, 8:9, :] = (from_up if row < 4 else from_down)[at : at + 1, :]
            set_factors(factors, coef, s, row, c)
        spans = ((1, SIDE + 7), (2, SIDE + 6), (3, SIDE + 5), (4, SIDE + 4))
        windows = ((4,), (5,), (6,), (8,)) if side == 0 else ((SIDE + 4,), (SIDE + 3,), (SIDE + 2,), (SIDE,))

        def store(half, row, c, value, side=side):
            done[side, half, row - 4, :, :] = value

        chain(s, x1, u, t, coef, store, spans, windows, 16)
        for half in range(2):
            copy = pltpu.make_async_copy(
                done.at[side, half],
                out.at[:, pl.ds(side * (SIDE - 8), 8), pl.ds(half * 128, 128)],
                sem_out.at[side, half],
            )
            copy.start()
            outs.append(copy)
    for copy in outs:
        copy.wait()


VMEM = pl.BlockSpec(memory_space=pltpu.VMEM)
HBM = pl.BlockSpec(memory_space=pltpu.HBM)
DMA = pltpu.SemaphoreType.DMA
FIELD = pltpu.VMEM((2, ROWS, COLS, 128), F32)
COEF = pltpu.VMEM((4, ROWS, COLS, 128), F32)
TURNED = pltpu.VMEM((COLS, 128), F32)
STATE = (FIELD, FIELD, FIELD, FIELD, COEF)


def call(kernel, in_specs, out_shape, out_specs, scratch, cost, grant, aliases=None):
    return pl.pallas_call(
        kernel,
        in_specs=in_specs,
        out_shape=out_shape,
        out_specs=out_specs,
        scratch_shapes=scratch,
        input_output_aliases=aliases or {},
        cost_estimate=pl.CostEstimate(flops=cost, bytes_accessed=1 << 20, transcendentals=0),
        compiler_params=pltpu.CompilerParams(vmem_limit_bytes=grant << 20),
    )


def block(east_class, south_class, cond_table, leakage, pad_mask, load):
    gx, gy = lax.axis_size("gx"), lax.axis_size("gy")

    def shift(values, axis, step):
        count = gx if axis == "gx" else gy
        return lax.ppermute(values, axis, [(i, (i + step) % count) for i in range(count)])

    potential = pltpu.HBM((SIDE, SIDE, 256), F32)
    given = [pltpu.with_memory_space_constraint(a, pltpu.HBM) for a in (cond_table, east_class, south_class, leakage, pad_mask, load)]
    to_right, to_left, to_down, to_up, te, ts, tx = call(
        pack_kernel,
        [HBM] * 6,
        [pltpu.VMEM((GY_MSG, 128), F32)] * 2 + [pltpu.VMEM((GX_MSG, 128), F32)] * 2 + [TURNED] * 3,
        [VMEM] * 7,
        [pltpu.SMEM((8,), F32)]
        + [pltpu.VMEM((SIDE, SIDE), kind) for kind in (jnp.int32, jnp.int32, F32, jnp.int32)]
        + [pltpu.VMEM((2, 2, SIDE, 8, 128), F32), DMA((2, 2)), DMA((2, 2, 4)), DMA((5,))],
        1 << 22,
        4,
    )(*given)
    from_left = shift(to_right, "gy", 1)
    from_up = shift(to_down, "gx", 1)
    from_down = shift(to_up, "gx", -1)
    from_right = shift(to_left, "gy", -1)
    *state, out = call(
        inner_kernel,
        [VMEM] * 3 + [HBM],
        [*STATE, potential],
        [VMEM] * 5 + [HBM],
        [pltpu.VMEM((2, SIDE, SIDE, 128), F32), DMA((4, 2)), DMA((2,))],
        1 << 25,
        6,
    )(te, ts, tx, given[5])
    corner_right, corner_left, te2, ts2, tx2 = call(
        corner_kernel, [VMEM] * 5, [pltpu.VMEM((CORNER_MSG, 128), F32)] * 2 + [TURNED] * 3, [VMEM] * 5, [], 1 << 20, 4
    )(te, ts, tx, from_up, from_down)
    corner_from_left = shift(corner_right, "gy", 1)
    corner_from_right = shift(corner_left, "gy", -1)
    *state, out = call(
        rows_kernel,
        [VMEM] * 11 + [HBM],
        [*STATE, potential],
        [VMEM] * 5 + [HBM],
        [pltpu.VMEM((2, 10, SIDE, 128), F32), DMA((2, 2))],
        1 << 24,
        4,
        {6 + i: i for i in range(6)},
    )(te2, ts2, tx2, from_up, from_down, to_up, *state, out)
    *state, out = call(
        sides_kernel,
        [VMEM] * 15 + [HBM],
        [*STATE, potential],
        [VMEM] * 5 + [HBM],
        [TURNED] * 3 + [pltpu.VMEM((2, 2, SIDE, 8, 128), F32), DMA((2, 2))],
        1 << 24,
        4,
        {10 + i: i for i in range(6)},
    )(te2, ts2, tx2, from_up, from_down, to_left, from_left, from_right, corner_from_left, corner_from_right, *state, out)
    return out


def solution(mesh):
    in_specs = (P("gx", "gy"), P("gx", "gy"), P(), P("gx", "gy"), P("gx", "gy"), P("gx", "gy", None))
    return jax.shard_map(block, mesh=mesh, in_specs=in_specs, out_specs=P("gx", "gy", None), check_vma=False)
```

time: 73.8 us -> 45 us (0.61)
  the two profiles are of different devices: /device:TPU:7 before, /device:TPU:8 now
where the time goes in v1:
time: 45 us; the launch traced here: 44.9 us
  Pallas kernels  23.7 us (53%)
  starting transfers between devices  18.2 us (40%)
  waiting for transfers between devices  2.84 us (6%)
    ppermute x6, starting transfers between devices, shift(): lax.ppermute(values, axis, [(i, (i + step) % count) for i in range(count)])  18.2 us
    pallas_call x1, Pallas kernels, block(): call(inner_kernel, [VMEM] * 3 + [HBM], [*STATE, potential], [VMEM] * 5 +...  14.5 us
    pallas_call x1, Pallas kernels, block(): call(sides_kernel, [VMEM] * 15 + [HBM], [*STATE, potential], [VMEM] * 5 +...  4.49 us
    ppermute x6, waiting for transfers between devices, shift(): lax.ppermute(values, axis, [(i, (i + step) % count) for i in range(count)])  2.84 us
    pallas_call x1, Pallas kernels, block(): call(rows_kernel, [VMEM] * 11 + [HBM], [*STATE, potential], [VMEM] * 5 +...  2.71 us
    pallas_call x1, Pallas kernels, block(): call(pack_kernel, [HBM] * 6, [pltpu.VMEM((GY_MSG, 128), F32)] * 2 + [pltp...  1.87 us
  transfers between devices with their start and end apart: 6, of which 1 were waited for; matrix products, arithmetic and copies ran while one was open for 0% of the time, Pallas kernels for 39%

profile of v1, /device:TPU:8, one launch (start us, length us, event | category | flops | bytes accessed | tf_op | source)
XLA Modules:
  0.0 44.9 jit_solution(8962312727903040699)
XLA Ops:
  0.0 1.9 %shard_map.64 = (f32[528,128]{1,0:T(8,128)S(1)}, f32[528,128]{1,0:T(8,128)S(1)}, f32[576,128]{1,0:T(8,128)S(1)}, f32[576,128]{1,0:T(8,128)S(1)}, f32[80,128]{1,0...) custom-call(f32[8]{0:T(128)} %refs_0_.1, s32[64,64]{1,0:T(8,128)} %refs_1_.1, s32[64,64]{1,0:T(8,128)} %refs_2_.1, ...), custom_call_target="tpu_custom_call" | custom-call | flops 4194304 | bytes 1048576 | tf_op jit(solution)/shard_map/pallas_call | solution.py:369
  1.9 2.2 %collective-permute-start.1 = (f32[576,128]{1,0:T(8,128)S(1)}, f32[576,128]{1,0:T(8,128)S(1)}, u32[]{:S(2)}, u32[]{:S(2)}) collective-permute-start(f32[576,128]{1,0:T(8,128)S(1)} %get-tuple-element.34.own_up), channel_id=1, source_target_pairs={{0,240},{16,0},{32,16},{48,32},{64,48},{80,64},{96,80},{112,96},{1... | collective-permute-start | bytes 884744 | tf_op jit(solution)/shard_map/ppermute | solution.py:365
  4.0 0.0 collective-permute-start
  4.0 7.9 %collective-permute-start.3 = (f32[528,128]{1,0:T(8,128)S(1)}, f32[528,128]{1,0:T(8,128)S(1)}, u32[]{:S(2)}, u32[]{:S(2)}) collective-permute-start(f32[528,128]{1,0:T(8,128)S(1)} %get-tuple-element.38.own_left), channel_id=1, source_target_pairs={{0,15},{1,0},{2,1},{3,2},{4,3},{5,4},{6,5},{7,6},{8,7},{9,8},{10,9... | collective-permute-start | bytes 811016 | tf_op jit(solution)/shard_map/ppermute | solution.py:365
  11.9 0.0 collective-permute-start.2
  11.9 0.0 collective-permute-done.1.from_down
  11.9 2.8 %collective-permute-done.from_up = f32[576,128]{1,0:T(8,128)S(1)} collective-permute-done((f32[576,128]{1,0:T(8,128)S(1)}, f32[576,128]{1,0:T(8,128)S(1)}, u32[]{:S(2)}, u32[]{:S(2)}) %collective-permute-start) | collective-permute-done | bytes 294944 | tf_op jit(solution)/shard_map/ppermute | solution.py:365
  14.8 0.1 shard_map.65
  14.9 0.3 collective-permute-start.4
  15.2 7.8 %collective-permute-start.5 = (f32[80,128]{1,0:T(8,128)S(1)}, f32[80,128]{1,0:T(8,128)S(1)}, u32[]{:S(2)}, u32[]{:S(2)}) collective-permute-start(f32[80,128]{1,0:T(8,128)S(1)} %get-tuple-element.41), channel_id=1, source_target_pairs={{0,15},{1,0},{2,1},{3,2},{4,3},{5,4},{6,5},{7,6},{8,7},{9,8},{10,9... | collective-permute-start | bytes 122888 | tf_op jit(solution)/shard_map/ppermute | solution.py:365
  23.0 14.5 %shard_map.66 = (f32[2,72,80,128]{3,2,1,0:T(8,128)S(1)}, f32[2,72,80,128]{3,2,1,0:T(8,128)S(1)}, f32[2,72,80,128]{3,2,1,0:T(8,128)S(1)}, f32[2,72,80,128]{3,2,1,...) custom-call(f32[80,128]{1,0:T(8,128)S(1)} %get-tuple-element.30.te, ...), custom_call_target="tpu_custom_call" | custom-call | flops 33554432 | bytes 1048576 | tf_op jit(solution)/shard_map/pallas_call | solution.py:384
  37.5 2.7 %shard_map.67 = (f32[2,72,80,128]{3,2,1,0:T(8,128)S(1)}, f32[2,72,80,128]{3,2,1,0:T(8,128)S(1)}, f32[2,72,80,128]{3,2,1,0:T(8,128)S(1)}, f32[2,72,80,128]{3,2,1,...) custom-call(f32[80,128]{1,0:T(8,128)S(1)} %get-tuple-element.35.te.t, ...), custom_call_target="tpu_custom_call", output_to_operand_aliasing={{0}: (6, {}), {1}: (7, {}), {2}: (8, {}), {3}: (9, {}), {4}... | custom-call | flops 16777216 | bytes 1048576 | tf_op jit(solution)/shard_map/pallas_call | solution.py:398
  40.2 0.0 collective-permute-done.3.from_right
  40.2 0.0 collective-permute-done.2.from_left
  40.2 0.0 collective-permute-done.4.corner_left
  40.3 0.0 collective-permute-done.5.corner_right
  40.3 4.5 %shard_map.68 = (f32[2,72,80,128]{3,2,1,0:T(8,128)S(1)}, f32[2,72,80,128]{3,2,1,0:T(8,128)S(1)}, f32[2,72,80,128]{3,2,1,0:T(8,128)S(1)}, f32[2,72,80,128]{3,2,1,...) custom-call(f32[80,128]{1,0:T(8,128)S(1)} %get-tuple-element.35.te.t, ...), custom_call_target="tpu_custom_call", output_to_operand_aliasing={{0}: (10, {}), {1}: (11, {}), {2}: (12, {}), {3}: (13, {}),... | custom-call | flops 16777216 | bytes 1048576 | tf_op jit(solution)/shard_map/pallas_call | solution.py:408
Async XLA Ops:
  1.9 10.1 %collective-permute-start.1 = (f32[576,128]{1,0:T(8,128)S(1)}, f32[576,128]{1,0:T(8,128)S(1)}, u32[]{:S(2)}, u32[]{:S(2)}) collective-permute-start(f32[576,128]{1,0:T(8,128)S(1)} %get-tuple-element.34.own_up), channel_id=1, source_target_pairs={{0,240},{16,0},{32,16},{48,32},{64,48},{80,64},{96,80},{112,96},{1... | collective-permute-start | bytes 884744 | tf_op jit(solution)/shard_map/ppermute | solution.py:365
  4.0 10.7 %collective-permute-start = (f32[576,128]{1,0:T(8,128)S(1)}, f32[576,128]{1,0:T(8,128)S(1)}, u32[]{:S(2)}, u32[]{:S(2)}) collective-permute-start(f32[576,128]{1,0:T(8,128)S(1)} %get-tuple-element.33), channel_id=1, source_target_pairs={{0,16},{16,32},{32,48},{48,64},{64,80},{80,96},{96,112},{112,128},... | collective-permute-start | bytes 884744 | tf_op jit(solution)/shard_map/ppermute | solution.py:365
  4.0 36.2 %collective-permute-start.3 = (f32[528,128]{1,0:T(8,128)S(1)}, f32[528,128]{1,0:T(8,128)S(1)}, u32[]{:S(2)}, u32[]{:S(2)}) collective-permute-start(f32[528,128]{1,0:T(8,128)S(1)} %get-tuple-element.38.own_left), channel_id=1, source_target_pairs={{0,15},{1,0},{2,1},{3,2},{4,3},{5,4},{6,5},{7,6},{8,7},{9,8},{10,9... | collective-permute-start | bytes 811016 | tf_op jit(solution)/shard_map/ppermute | solution.py:365
  11.9 28.3 %collective-permute-start.2 = (f32[528,128]{1,0:T(8,128)S(1)}, f32[528,128]{1,0:T(8,128)S(1)}, u32[]{:S(2)}, u32[]{:S(2)}) collective-permute-start(f32[528,128]{1,0:T(8,128)S(1)} %get-tuple-element.39), channel_id=1, source_target_pairs={{0,1},{1,2},{2,3},{3,4},{4,5},{5,6},{6,7},{7,8},{8,9},{9,10},{10,1... | collective-permute-start | bytes 811016 | tf_op jit(solution)/shard_map/ppermute | solution.py:365
  14.9 25.4 %collective-permute-start.4 = (f32[80,128]{1,0:T(8,128)S(1)}, f32[80,128]{1,0:T(8,128)S(1)}, u32[]{:S(2)}, u32[]{:S(2)}) collective-permute-start(f32[80,128]{1,0:T(8,128)S(1)} %get-tuple-element.40), channel_id=1, source_target_pairs={{0,1},{1,2},{2,3},{3,4},{4,5},{5,6},{6,7},{7,8},{8,9},{9,10},{10,1... | collective-permute-start | bytes 122888 | tf_op jit(solution)/shard_map/ppermute | solution.py:365
  15.2 25.1 %collective-permute-start.5 = (f32[80,128]{1,0:T(8,128)S(1)}, f32[80,128]{1,0:T(8,128)S(1)}, u32[]{:S(2)}, u32[]{:S(2)}) collective-permute-start(f32[80,128]{1,0:T(8,128)S(1)} %get-tuple-element.41), channel_id=1, source_target_pairs={{0,15},{1,0},{2,1},{3,2},{4,3},{5,4},{6,5},{7,6},{8,7},{9,8},{10,9... | collective-permute-start | bytes 122888 | tf_op jit(solution)/shard_map/ppermute | solution.py:365

commit v2 on v1

v2 whole, which is shorter than its diff:
```python
import jax
import jax.numpy as jnp
from jax import lax
from jax.experimental import pallas as pl
from jax.experimental.pallas import tpu as pltpu
from jax.sharding import PartitionSpec as P


PAD_GAIN = 8.0
SPECTRAL_BOUND = 0.995


SIDE = 64
ROWS = SIDE + 8
COLS = SIDE + 16
GX_MSG = 8 * SIDE + SIDE
GY_MSG = 8 * SIDE
CORNER_MSG = 24 + 16
TURNED_ROWS = SIDE + 24
F32 = jnp.float32


def weights():
    b2 = SPECTRAL_BOUND * SPECTRAL_BOUND
    first = 1.0 / (1.0 - b2 / 2.0)
    second = 1.0 / (1.0 - b2 * first / 4.0)
    third = 1.0 / (1.0 - b2 * second / 4.0)
    return first, second, third


W1, W2, W3 = weights()
MIX = W3 + (1.0 - W3) * W1
TOP = W1 * W2 * W3


EAST, SOUTH, ROOT, FIXED = range(4)


def lanes_of(shape):
    return lax.broadcasted_iota(jnp.int32, shape, 1)


def turn_factors(te, ts, tx, factors, roots, easts, souths):
    for k in roots:
        south = ts[k : k + 8, :]
        ground = tx[k : k + 8, :]
        diagonal = te[k : k + 8, :] + te[k - 1 : k + 7, :] + south + pltpu.roll(south, 1, 1) + ground
        root = 1.0 / jnp.sqrt(diagonal)
        factors[ROOT, k : k + 8, :] = root
        factors[FIXED, k : k + 8, :] = jnp.where(ground > 4.0, PAD_GAIN, 0.0) * root
    for k in easts:
        factors[EAST, k : k + 8, :] = te[k : k + 8, :] * factors[ROOT, k : k + 8, :] * factors[ROOT, k + 1 : k + 9, :]
    for k in souths:
        root = factors[ROOT, k : k + 8, :]
        factors[SOUTH, k : k + 8, :] = ts[k : k + 8, :] * root * pltpu.roll(root, 127, 1)


def spread(values, lane):
    return jnp.broadcast_to(values[:, lane : lane + 1], (8, 128))


def to_source(s, row, c, fixed, root):
    for half in range(2):
        s[half, row, pl.ds(c, 8), :] = fixed - s[half, row, pl.ds(c, 8), :] * root


def neighbours(src, coef, base, count, c, emit):
    above = [src[half, base - 1, pl.ds(c, 8), :] for half in range(2)]
    here = [src[half, base, pl.ds(c, 8), :] for half in range(2)]
    north = coef[SOUTH, base - 1, pl.ds(c, 8), :]
    for step in range(count):
        row = base + step
        east = coef[EAST, row, pl.ds(c, 8), :]
        west = coef[EAST, row, pl.ds(c - 1, 8), :]
        south = coef[SOUTH, row, pl.ds(c, 8), :]
        for half in range(2):
            below = src[half, row + 1, pl.ds(c, 8), :]
            total = east * src[half, row, pl.ds(c + 1, 8), :] + west * src[half, row, pl.ds(c - 1, 8), :]
            total = total + (south * below + north * above[half])
            emit(half, row, c, total, here[half])
            above[half], here[half] = here[half], below
        north = south


def sweep(src, coef, first, last, columns, unroll, emit):
    full = (last - first) // unroll
    for c in columns:
        if full == 1:
            neighbours(src, coef, first, unroll, c, emit)
        elif full > 1:

            def trip(index, carry, c=c):
                neighbours(src, coef, first + index * unroll, unroll, c, emit)
                return carry

            lax.fori_loop(0, full, trip, 0)
        if first + full * unroll < last:
            neighbours(src, coef, first + full * unroll, last - first - full * unroll, c, emit)


def adding(target):
    def emit(half, row, c, total, here):
        target[half, row, pl.ds(c, 8), :] = here + total

    return emit


def placing(target):
    def emit(half, row, c, total, here):
        target[half, row, pl.ds(c, 8), :] = total

    return emit


def result(s, u, coef, half, row, c, total):
    value = s[half, row, pl.ds(c, 8), :] + (MIX * u[half, row, pl.ds(c, 8), :] + TOP * total)
    return value * coef[ROOT, row, pl.ds(c, 8), :]


def pack_kernel(*refs):
    small, load = refs[:5], refs[5]
    to_right, to_left, to_down, to_up, te, ts, tx = refs[6:13]
    edge, sem_edge, sem_rows, sem_small = refs[18:]
    table, east_class, south_class, leakage, pad_mask = refs[13:18]
    edges, tops = [], []
    nodes = [pltpu.make_async_copy(source, target, sem_small.at[i]) for i, (source, target) in enumerate(zip(small, refs[13:18]))]
    for copy in nodes:
        copy.start()
    for side in range(2):
        for half in range(2):
            copy = pltpu.make_async_copy(
                load.at[:, pl.ds(side * (SIDE - 8), 8), pl.ds(half * 128, 128)], edge.at[side, half], sem_edge.at[side, half]
            )
            copy.start()
            edges.append(copy)
    for side, message in enumerate((to_up, to_down)):
        for half in range(2):
            for row in range(4):
                copy = pltpu.make_async_copy(
                    load.at[side * (SIDE - 4) + row, :, pl.ds(half * 128, 128)],
                    message.at[pl.ds((half * 4 + row) * SIDE, SIDE), :],
                    sem_rows.at[side, half, row],
                )
                copy.start()
                tops.append(copy)

    for copy in nodes:
        copy.wait()

    def look_up(classes):
        found = jnp.zeros((SIDE, SIDE), F32)
        for label in range(8):
            found = jnp.where(classes == label, table[label], found)
        return found

    zeros = jnp.zeros((SIDE, 128 - SIDE), F32)

    def turned(values):
        return pltpu.roll(jnp.concatenate([values.T, zeros], axis=1), 8, 1)

    east = turned(look_up(east_class[...]))
    south = turned(look_up(south_class[...]))
    ground = turned(leakage[...] + PAD_GAIN * pad_mask[...].astype(F32))
    for target, values in ((te, east), (ts, south), (tx, ground)):
        target[0:8, :] = jnp.zeros((8, 128), F32)
        target[8 : SIDE + 8, :] = values
        target[SIDE + 8 :, :] = jnp.zeros((16, 128), F32)
    lane = lanes_of((SIDE, 128))

    def banded(shifts):
        first, second, third = [
            values if shift == 0 else pltpu.roll(values, shift, 1) for values, shift in zip((east, south, ground), shifts)
        ]
        return jnp.where(lane < 8, first, jnp.where(lane < 16, second, third))

    to_down[8 * SIDE :, :] = banded((64, 72, 80))
    to_up[8 * SIDE :, :] = banded((120, 0, 8))
    for copy in edges:
        copy.wait()
    for side, message in enumerate((to_left, to_right)):
        for half in range(2):
            for row in range(SIDE):
                base = (half * SIDE + row) * 4
                message[base : base + 4, :] = edge[side, half, row, side * 4 : side * 4 + 4, :]
    for copy in tops:
        copy.wait()


def put_conductances(message, base, te, ts, tx, first_east, first_other):
    message[base : base + 5, :] = te[first_east : first_east + 5, :]
    message[base + 5 : base + 9, :] = ts[first_other : first_other + 4, :]
    message[base + 9 : base + 13, :] = tx[first_other : first_other + 4, :]
    message[base + 13 : base + 16, :] = jnp.zeros((3, 128), F32)


def first_kernel(te, ts, tx, load, s, x1, coef, factors, sem):
    def part(group, half):
        return pltpu.make_async_copy(
            load.at[pl.ds(group * 8, 8), :, pl.ds(half * 128, 128)],
            s.at[half, pl.ds(4 + group * 8, 8), pl.ds(8, SIDE), :],
            sem.at[group, half],
        )

    for group in range(SIDE // 8):
        for half in range(2):
            part(group, half).start()
    own = range(8, SIDE + 8, 8)
    turn_factors(te, ts, tx, factors, own, own, own)

    def body(group, carry):
        for half in range(2):
            part(group, half).wait()
        for step in range(8):
            row = group * 8 + 4 + step
            for c in own:
                values = [spread(factors[which, c : c + 8, :], 8 + step) for which in range(4)]
                for which in (EAST, SOUTH, ROOT):
                    coef[which, row, c : c + 8, :] = values[which]
                to_source(s, row, c, values[FIXED], values[ROOT])
        for c in own:
            neighbours(s, coef, group * 8 + 3, 8, c, adding(x1))
            for which in range(4):
                factors[which, c : c + 8, :] = pltpu.roll(factors[which, c : c + 8, :], 120, 1)
        return carry

    lax.fori_loop(0, SIDE // 8, body, 0)


def corner_cells():
    for half in range(2):
        for side in range(2):
            for distance in (1, 2, 3):
                yield (half * 2 + side) * 6 + (0, 3, 5)[distance - 1], half, side, distance


def corner_kernel(te, ts, tx, from_up, from_down, to_right, to_left, te2, ts2, tx2):
    lane = lanes_of((SIDE, 128))
    upper, lower = from_up[8 * SIDE :, :], from_down[8 * SIDE :, :]
    for source, target, down, up in ((te, te2, 0, 72), (ts, ts2, 120, 64), (tx, tx2, 112, 56)):
        head = pltpu.roll(upper, down, 1) if down else upper
        tail = pltpu.roll(lower, up, 1)
        own = source[8 : SIDE + 8, :]
        target[0:8, :] = jnp.zeros((8, 128), F32)
        target[8 : SIDE + 8, :] = jnp.where(lane < 8, head, jnp.where(lane < SIDE + 8, own, tail))
        target[SIDE + 8 :, :] = jnp.zeros((16, 128), F32)
    for offset, half, side, distance in corner_cells():
        count = 4 - distance
        origin, row = (from_down, distance - 1) if side else (from_up, 4 - distance)
        at = (half * 4 + row) * SIDE
        to_right[offset : offset + count, :] = origin[at + SIDE - count : at + SIDE, :]
        to_left[offset : offset + count, :] = origin[at : at + count, :]
    put_conductances(to_right, 24, te2, ts2, tx2, SIDE + 3, SIDE + 4)
    put_conductances(to_left, 24, te2, ts2, tx2, 8, 8)


def main_kernel(te, ts, tx, from_up, from_down, own_up, *rest):
    s, x1, coef, u, t, out, factors, done, sem = rest[3:]
    own = range(8, SIDE + 8, 8)
    turn_factors(te, ts, tx, factors, own, own, own)
    for half in range(2):
        for row in range(4):
            at = (half * 4 + row) * SIDE
            s[half, row, 8 : SIDE + 8, :] = from_up[at : at + SIDE, :]
            s[half, SIDE + 4 + row, 8 : SIDE + 8, :] = from_down[at : at + SIDE, :]
        s[half, 4, 8 : SIDE + 8, :] = own_up[half * 4 * SIDE : half * 4 * SIDE + SIDE, :]
    for row in (0, 1, 2, 3, 4, SIDE + 3, SIDE + 4, SIDE + 5, SIDE + 6, SIDE + 7):
        for c in own:
            values = [spread(factors[which, c : c + 8, :], row + 4) for which in range(4)]
            for which in (EAST, SOUTH, ROOT):
                coef[which, row, c : c + 8, :] = values[which]
            if row != SIDE + 3:
                to_source(s, row, c, values[FIXED], values[ROOT])
    sweep(s, coef, 1, 6, own, 5, adding(x1))
    sweep(s, coef, SIDE + 3, SIDE + 7, own, 4, adding(x1))
    sweep(x1, coef, 2, SIDE + 6, own, 17, placing(u))
    sweep(u, coef, 3, SIDE + 5, own, 22, placing(t))

    def finish(half, row, c, total, here):
        done[half, row - 4, c - 8 : c, :] = result(s, u, coef, half, row, c, total)

    outs = []
    for part in range(4):
        rows = pl.ds(part * 16, 16)
        sweep(t, coef, 4 + part * 16, 20 + part * 16, range(16, SIDE, 8), 16, finish)
        for half in range(2):
            copy = pltpu.make_async_copy(
                done.at[half, rows, pl.ds(8, SIDE - 16), :],
                out.at[rows, pl.ds(8, SIDE - 16), pl.ds(half * 128, 128)],
                sem.at[part, half],
            )
            copy.start()
            outs.append(copy)
    for copy in outs:
        copy.wait()


def sides_kernel(te2, ts2, tx2, from_up, from_down, own_left, from_left, from_right, corner_left, corner_right, *rest):
    s, x1, coef, u, t, out, te, ts, tx, factors, done, sem = rest[6:]
    for source, target in ((te2, te), (ts2, ts), (tx2, tx)):
        target[...] = source[...]
    for corner, first_east, first_other in ((corner_left, 3, 4), (corner_right, SIDE + 8, SIDE + 8)):
        te[first_east : first_east + 5, :] = corner[24:29, :]
        ts[first_other : first_other + 4, :] = corner[29:33, :]
        tx[first_other : first_other + 4, :] = corner[33:37, :]
    turn_factors(te, ts, tx, factors, (1, 8, SIDE, SIDE + 8), (1, SIDE + 7), (1, SIDE + 8))

    def unpack(index, carry):
        for step in range(8):
            row = index * 8 + step
            for half in range(2):
                at = (half * SIDE + row) * 4
                s[half, row + 4, 4:8, :] = from_left[pl.ds(at, 4), :]
                s[half, row + 4, 8:9, :] = own_left[pl.ds(at, 1), :]
                s[half, row + 4, SIDE + 8 : SIDE + 12, :] = from_right[pl.ds(at, 4), :]
        return carry

    lax.fori_loop(0, SIDE // 8, unpack, 0)
    for half in range(2):
        for row in range(4):
            at = (half * 4 + row) * SIDE
            s[half, row, 8:9, :] = from_up[at : at + 1, :]
            s[half, SIDE + 4 + row, 8:9, :] = from_down[at : at + 1, :]
    for offset, half, side, distance in corner_cells():
        count = 4 - distance
        row = SIDE + 3 + distance if side else 4 - distance
        s[half, row, 8 - count : 8, :] = corner_left[offset : offset + count, :]
        s[half, row, SIDE + 8 : SIDE + 8 + count, :] = corner_right[offset : offset + count, :]
    used = [(which, 1) for which in range(4)] + [(EAST, SIDE + 7)] + [(which, SIDE + 8) for which in (SOUTH, ROOT, FIXED)]

    def body(group, carry):
        for step in range(8):
            row = group * 8 + step
            values = [spread(factors[which, c : c + 8, :], 4 + step) for which, c in used]
            for (which, c), value in zip(used, values):
                if which != FIXED:
                    coef[which, row, c : c + 8, :] = value
            to_source(s, row, 1, values[FIXED], values[ROOT])
            to_source(s, row, SIDE + 8, values[7], values[6])
        for which, c in used:
            factors[which, c : c + 8, :] = pltpu.roll(factors[which, c : c + 8, :], 120, 1)
        return carry

    lax.fori_loop(0, ROWS // 8, body, 0)
    sweep(s, coef, 1, SIDE + 7, (4, SIDE + 4), 14, adding(x1))
    sweep(x1, coef, 2, SIDE + 6, (5, SIDE + 3), 17, placing(u))
    sweep(u, coef, 3, SIDE + 5, (6, SIDE + 2), 22, placing(t))
    outs = []
    for side in range(2):

        def finish(half, row, c, total, here, side=side):
            done[side, half, row - 4, :, :] = result(s, u, coef, half, row, c, total)

        sweep(t, coef, 4, SIDE + 4, ((8, SIDE)[side],), 16, finish)
        for half in range(2):
            copy = pltpu.make_async_copy(
                done.at[side, half],
                out.at[:, pl.ds(side * (SIDE - 8), 8), pl.ds(half * 128, 128)],
                sem.at[side, half],
            )
            copy.start()
            outs.append(copy)
    for copy in outs:
        copy.wait()


VMEM = pl.BlockSpec(memory_space=pltpu.VMEM)
HBM = pl.BlockSpec(memory_space=pltpu.HBM)
DMA = pltpu.SemaphoreType.DMA
FIELD = pltpu.VMEM((2, ROWS, COLS, 128), F32)
COEF = pltpu.VMEM((3, ROWS, COLS, 128), F32)
TURNED = pltpu.VMEM((TURNED_ROWS, 128), F32)
FACTORS = pltpu.VMEM((4, TURNED_ROWS, 128), F32)


def call(kernel, in_specs, out_shape, out_specs, scratch, cost, grant, aliases=None):
    return pl.pallas_call(
        kernel,
        in_specs=in_specs,
        out_shape=out_shape,
        out_specs=out_specs,
        scratch_shapes=scratch,
        input_output_aliases=aliases or {},
        cost_estimate=pl.CostEstimate(flops=cost, bytes_accessed=1 << 20, transcendentals=0),
        compiler_params=pltpu.CompilerParams(vmem_limit_bytes=grant << 20),
    )


def block(east_class, south_class, cond_table, leakage, pad_mask, load):
    gx, gy = lax.axis_size("gx"), lax.axis_size("gy")

    def shift(values, axis, step):
        count = gx if axis == "gx" else gy
        return lax.ppermute(values, axis, [(i, (i + step) % count) for i in range(count)])

    potential = pltpu.HBM((SIDE, SIDE, 256), F32)
    given = [pltpu.with_memory_space_constraint(a, pltpu.HBM) for a in (cond_table, east_class, south_class, leakage, pad_mask, load)]
    to_right, to_left, to_down, to_up, te, ts, tx = call(
        pack_kernel,
        [HBM] * 6,
        [pltpu.VMEM((GY_MSG, 128), F32)] * 2 + [pltpu.VMEM((GX_MSG, 128), F32)] * 2 + [TURNED] * 3,
        [VMEM] * 7,
        [pltpu.SMEM((8,), F32)]
        + [pltpu.VMEM((SIDE, SIDE), kind) for kind in (jnp.int32, jnp.int32, F32, jnp.int32)]
        + [pltpu.VMEM((2, 2, SIDE, 8, 128), F32), DMA((2, 2)), DMA((2, 2, 4)), DMA((5,))],
        1 << 22,
        4,
    )(*given)
    from_left = shift(to_right, "gy", 1)
    from_right = shift(to_left, "gy", -1)
    from_up = shift(to_down, "gx", 1)
    from_down = shift(to_up, "gx", -1)
    s, x1, coef = call(
        first_kernel, [VMEM] * 3 + [HBM], [FIELD, FIELD, COEF], [VMEM] * 3, [FACTORS, DMA((SIDE // 8, 2))], 1 << 25, 4
    )(te, ts, tx, given[5])
    corner_right, corner_left, te2, ts2, tx2 = call(
        corner_kernel, [VMEM] * 5, [pltpu.VMEM((CORNER_MSG, 128), F32)] * 2 + [TURNED] * 3, [VMEM] * 5, [], 1 << 20, 4
    )(te, ts, tx, from_up, from_down)
    corner_from_left = shift(corner_right, "gy", 1)
    corner_from_right = shift(corner_left, "gy", -1)
    *state, out = call(
        main_kernel,
        [VMEM] * 9,
        [FIELD, FIELD, COEF, FIELD, FIELD, potential],
        [VMEM] * 5 + [HBM],
        [FACTORS, pltpu.VMEM((2, SIDE, SIDE, 128), F32), DMA((4, 2))],
        1 << 25,
        6,
        {6 + i: i for i in range(3)},
    )(te2, ts2, tx2, from_up, from_down, to_up, s, x1, coef)
    *state, out = call(
        sides_kernel,
        [VMEM] * 15 + [HBM],
        [FIELD, FIELD, COEF, FIELD, FIELD, potential],
        [VMEM] * 5 + [HBM],
        [TURNED] * 3 + [FACTORS, pltpu.VMEM((2, 2, SIDE, 8, 128), F32), DMA((2, 2))],
        1 << 24,
        4,
        {10 + i: i for i in range(6)},
    )(te2, ts2, tx2, from_up, from_down, to_left, from_left, from_right, corner_from_left, corner_from_right, *state, out)
    return out


def solution(mesh):
    in_specs = (P("gx", "gy"), P("gx", "gy"), P(), P("gx", "gy"), P("gx", "gy"), P("gx", "gy", None))
    return jax.shard_map(block, mesh=mesh, in_specs=in_specs, out_specs=P("gx", "gy", None), check_vma=False)
```

time: 45 us -> 37.4 us (0.83)
  the two profiles are of different devices: /device:TPU:8 before, /device:TPU:7 now
where the time goes in v2:
time: 37.4 us; the launch traced here: 37.3 us
  starting transfers between devices  18.8 us (50%)
  Pallas kernels  16.7 us (45%)
  waiting for transfers between devices  1.82 us (5%)
    ppermute x6, starting transfers between devices, shift(): lax.ppermute(values, axis, [(i, (i + step) % count) for i in range(count)])  18.8 us
    pallas_call x1, Pallas kernels, block(): call(main_kernel, [VMEM] * 9, [FIELD, FIELD, COEF, FIELD, FIELD, potentia...  5.92 us
    pallas_call x1, Pallas kernels, block(): call(first_kernel, [VMEM] * 3 + [HBM], [FIELD, FIELD, COEF], [VMEM] * 3,...  4.45 us
    pallas_call x1, Pallas kernels, block(): call(sides_kernel, [VMEM] * 15 + [HBM], [FIELD, FIELD, COEF, FIELD, FIELD...  4.32 us
    pallas_call x1, Pallas kernels, block(): call(pack_kernel, [HBM] * 6, [pltpu.VMEM((GY_MSG, 128), F32)] * 2 + [pltp...  1.87 us
    ppermute x6, waiting for transfers between devices, shift(): lax.ppermute(values, axis, [(i, (i + step) % count) for i in range(count)])  1.82 us
  transfers between devices with their start and end apart: 6, of which 1 were waited for; matrix products, arithmetic and copies ran while one was open for 0% of the time, Pallas kernels for 28%

profile of v2, /device:TPU:7, one launch (start us, length us, event | category | flops | bytes accessed | tf_op | source)
XLA Modules:
  0.0 37.3 jit_solution(13227477566788172753)
XLA Ops:
  0.0 1.9 %shard_map.64 = (f32[512,128]{1,0:T(8,128)S(1)}, f32[512,128]{1,0:T(8,128)S(1)}, f32[576,128]{1,0:T(8,128)S(1)}, f32[576,128]{1,0:T(8,128)S(1)}, f32[88,128]{1,0...) custom-call(f32[8]{0:T(128)} %refs_0_.1, s32[64,64]{1,0:T(8,128)} %refs_1_.1, s32[64,64]{1,0:T(8,128)} %refs_2_.1, ...), custom_call_target="tpu_custom_call" | custom-call | flops 4194304 | bytes 1048576 | tf_op jit(solution)/shard_map/pallas_call | solution.py:397
  1.9 1.8 %collective-permute-start = (f32[576,128]{1,0:T(8,128)S(1)}, f32[576,128]{1,0:T(8,128)S(1)}, u32[]{:S(2)}, u32[]{:S(2)}) collective-permute-start(f32[576,128]{1,0:T(8,128)S(1)} %get-tuple-element.30), channel_id=1, source_target_pairs={{0,16},{16,32},{32,48},{48,64},{64,80},{80,96},{96,112},{112,128},... | collective-permute-start | bytes 884744 | tf_op jit(solution)/shard_map/ppermute | solution.py:393
  3.7 0.0 collective-permute-start.1
  3.7 2.6 %collective-permute-start.2 = (f32[512,128]{1,0:T(8,128)S(1)}, f32[512,128]{1,0:T(8,128)S(1)}, u32[]{:S(2)}, u32[]{:S(2)}) collective-permute-start(f32[512,128]{1,0:T(8,128)S(1)} %get-tuple-element.36), channel_id=1, source_target_pairs={{0,1},{1,2},{2,3},{3,4},{4,5},{5,6},{6,7},{7,8},{8,9},{9,10},{10,1... | collective-permute-start | bytes 786440 | tf_op jit(solution)/shard_map/ppermute | solution.py:393
  6.4 5.3 %collective-permute-start.3 = (f32[512,128]{1,0:T(8,128)S(1)}, f32[512,128]{1,0:T(8,128)S(1)}, u32[]{:S(2)}, u32[]{:S(2)}) collective-permute-start(f32[512,128]{1,0:T(8,128)S(1)} %get-tuple-element.35.own_left), channel_id=1, source_target_pairs={{0,15},{1,0},{2,1},{3,2},{4,3},{5,4},{6,5},{7,6},{8,7},{9,8},{10,9... | collective-permute-start | bytes 786440 | tf_op jit(solution)/shard_map/ppermute | solution.py:393
  11.6 0.0 collective-permute-done.from_up
  11.7 1.8 %collective-permute-done.1.from_down = f32[576,128]{1,0:T(8,128)S(1)} collective-permute-done((f32[576,128]{1,0:T(8,128)S(1)}, f32[576,128]{1,0:T(8,128)S(1)}, u32[]{:S(2)}, u32[]{:S(2)}) %collective-permute-start.1) | collective-permute-done | bytes 294944 | tf_op jit(solution)/shard_map/ppermute | solution.py:393
  13.5 0.1 shard_map.65
  13.6 2.9 %collective-permute-start.4 = (f32[40,128]{1,0:T(8,128)S(1)}, f32[40,128]{1,0:T(8,128)S(1)}, u32[]{:S(2)}, u32[]{:S(2)}) collective-permute-start(f32[40,128]{1,0:T(8,128)S(1)} %get-tuple-element.37), channel_id=1, source_target_pairs={{0,1},{1,2},{2,3},{3,4},{4,5},{5,6},{6,7},{7,8},{8,9},{9,10},{10,1... | collective-permute-start | bytes 61448 | tf_op jit(solution)/shard_map/ppermute | solution.py:393
  16.5 6.1 %collective-permute-start.5 = (f32[40,128]{1,0:T(8,128)S(1)}, f32[40,128]{1,0:T(8,128)S(1)}, u32[]{:S(2)}, u32[]{:S(2)}) collective-permute-start(f32[40,128]{1,0:T(8,128)S(1)} %get-tuple-element.38), channel_id=1, source_target_pairs={{0,15},{1,0},{2,1},{3,2},{4,3},{5,4},{6,5},{7,6},{8,7},{9,8},{10,9... | collective-permute-start | bytes 61448 | tf_op jit(solution)/shard_map/ppermute | solution.py:393
  22.6 4.5 %shard_map.66 = (f32[2,72,80,128]{3,2,1,0:T(8,128)S(1)}, f32[2,72,80,128]{3,2,1,0:T(8,128)S(1)}, f32[3,72,80,128]{3,2,1,0:T(8,128)S(1)}) custom-call(f32[88,128]{1,0:T(8,128)S(1)} %get-tuple-element.27.te, f32[88,128]{1,0:T(8,128)S(1)} %get-tuple-element.28.ts, f32[88,128]{1,0:T(8,128)S(1)} %get-tuple-element.29.tx, f32[64,64,256]{2,1,0:T(8,128)} %load.1), custom_call_target="tpu_custom_call" | custom-call | flops 33554432 | bytes 1048576 | tf_op jit(solution)/shard_map/pallas_call | solution.py:412
  27.1 5.9 %shard_map.67 = (f32[2,72,80,128]{3,2,1,0:T(8,128)S(1)}, f32[2,72,80,128]{3,2,1,0:T(8,128)S(1)}, f32[3,72,80,128]{3,2,1,0:T(8,128)S(1)}, f32[2,72,80,128]{3,2,1,...) custom-call(f32[88,128]{1,0:T(8,128)S(1)} %get-tuple-element.32.te.t, ...), custom_call_target="tpu_custom_call", output_to_operand_aliasing={{0}: (6, {}), {1}: (7, {}), {2}: (8, {})} | custom-call | flops 33554432 | bytes 1048576 | tf_op jit(solution)/shard_map/pallas_call | solution.py:420
  33.0 0.0 collective-permute-done.2.from_left
  33.0 0.0 collective-permute-done.3.from_right
  33.0 0.0 collective-permute-done.4.corner_left
  33.0 0.0 collective-permute-done.5.corner_right
  33.0 4.3 %shard_map.68 = (f32[2,72,80,128]{3,2,1,0:T(8,128)S(1)}, f32[2,72,80,128]{3,2,1,0:T(8,128)S(1)}, f32[3,72,80,128]{3,2,1,0:T(8,128)S(1)}, f32[2,72,80,128]{3,2,1,...) custom-call(f32[88,128]{1,0:T(8,128)S(1)} %get-tuple-element.32.te.t, ...), custom_call_target="tpu_custom_call", output_to_operand_aliasing={{0}: (10, {}), {1}: (11, {}), {2}: (12, {}), {3}: (13, {}),... | custom-call | flops 16777216 | bytes 1048576 | tf_op jit(solution)/shard_map/pallas_call | solution.py:430
Async XLA Ops:
  1.9 9.8 %collective-permute-start = (f32[576,128]{1,0:T(8,128)S(1)}, f32[576,128]{1,0:T(8,128)S(1)}, u32[]{:S(2)}, u32[]{:S(2)}) collective-permute-start(f32[576,128]{1,0:T(8,128)S(1)} %get-tuple-element.30), channel_id=1, source_target_pairs={{0,16},{16,32},{32,48},{48,64},{64,80},{80,96},{96,112},{112,128},... | collective-permute-start | bytes 884744 | tf_op jit(solution)/shard_map/ppermute | solution.py:393
  3.7 9.7 %collective-permute-start.1 = (f32[576,128]{1,0:T(8,128)S(1)}, f32[576,128]{1,0:T(8,128)S(1)}, u32[]{:S(2)}, u32[]{:S(2)}) collective-permute-start(f32[576,128]{1,0:T(8,128)S(1)} %get-tuple-element.31.own_up), channel_id=1, source_target_pairs={{0,240},{16,0},{32,16},{48,32},{64,48},{80,64},{96,80},{112,96},{1... | collective-permute-start | bytes 884744 | tf_op jit(solution)/shard_map/ppermute | solution.py:393
  3.7 29.3 %collective-permute-start.2 = (f32[512,128]{1,0:T(8,128)S(1)}, f32[512,128]{1,0:T(8,128)S(1)}, u32[]{:S(2)}, u32[]{:S(2)}) collective-permute-start(f32[512,128]{1,0:T(8,128)S(1)} %get-tuple-element.36), channel_id=1, source_target_pairs={{0,1},{1,2},{2,3},{3,4},{4,5},{5,6},{6,7},{7,8},{8,9},{9,10},{10,1... | collective-permute-start | bytes 786440 | tf_op jit(solution)/shard_map/ppermute | solution.py:393
  6.4 26.6 %collective-permute-start.3 = (f32[512,128]{1,0:T(8,128)S(1)}, f32[512,128]{1,0:T(8,128)S(1)}, u32[]{:S(2)}, u32[]{:S(2)}) collective-permute-start(f32[512,128]{1,0:T(8,128)S(1)} %get-tuple-element.35.own_left), channel_id=1, source_target_pairs={{0,15},{1,0},{2,1},{3,2},{4,3},{5,4},{6,5},{7,6},{8,7},{9,8},{10,9... | collective-permute-start | bytes 786440 | tf_op jit(solution)/shard_map/ppermute | solution.py:393
  13.6 19.4 %collective-permute-start.4 = (f32[40,128]{1,0:T(8,128)S(1)}, f32[40,128]{1,0:T(8,128)S(1)}, u32[]{:S(2)}, u32[]{:S(2)}) collective-permute-start(f32[40,128]{1,0:T(8,128)S(1)} %get-tuple-element.37), channel_id=1, source_target_pairs={{0,1},{1,2},{2,3},{3,4},{4,5},{5,6},{6,7},{7,8},{8,9},{9,10},{10,1... | collective-permute-start | bytes 61448 | tf_op jit(solution)/shard_map/ppermute | solution.py:393
  16.5 16.5 %collective-permute-start.5 = (f32[40,128]{1,0:T(8,128)S(1)}, f32[40,128]{1,0:T(8,128)S(1)}, u32[]{:S(2)}, u32[]{:S(2)}) collective-permute-start(f32[40,128]{1,0:T(8,128)S(1)} %get-tuple-element.38), channel_id=1, source_target_pairs={{0,15},{1,0},{2,1},{3,2},{4,3},{5,4},{6,5},{7,6},{8,7},{9,8},{10,9... | collective-permute-start | bytes 61448 | tf_op jit(solution)/shard_map/ppermute | solution.py:393

commit v3 on v2

v3 whole, which is shorter than its diff:
```python
import functools

import jax
import jax.numpy as jnp
from jax import lax
from jax.experimental import pallas as pl
from jax.experimental.pallas import tpu as pltpu
from jax.sharding import PartitionSpec as P


PAD_GAIN = 8.0
SPECTRAL_BOUND = 0.995


SIDE = 64
ROWS = SIDE + 8
COLS = SIDE + 16
MAIN_MSG = 8 * SIDE
TINY_MSG = SIDE + 24
FULL_MSG = MAIN_MSG + 24 + 16
TURNED_ROWS = SIDE + 24
F32 = jnp.float32


def weights():
    b2 = SPECTRAL_BOUND * SPECTRAL_BOUND
    first = 1.0 / (1.0 - b2 / 2.0)
    second = 1.0 / (1.0 - b2 * first / 4.0)
    third = 1.0 / (1.0 - b2 * second / 4.0)
    return first, second, third


W1, W2, W3 = weights()
MIX = W3 + (1.0 - W3) * W1
TOP = W1 * W2 * W3


EAST, SOUTH, ROOT = range(3)


def lanes_of(shape):
    return lax.broadcasted_iota(jnp.int32, shape, 1)


def turn_factors(te, ts, tx, factors, roots, easts, souths):
    for k in roots:
        south = ts[k : k + 8, :]
        ground = tx[k : k + 8, :]
        diagonal = te[k : k + 8, :] + te[k - 1 : k + 7, :] + south + pltpu.roll(south, 1, 1) + ground
        root = 1.0 / jnp.sqrt(diagonal)
        factors[ROOT, k : k + 8, :] = jnp.where(ground > 4.0, -root, root)
    for k in easts:
        factors[EAST, k : k + 8, :] = te[k : k + 8, :] * jnp.abs(factors[ROOT, k : k + 8, :] * factors[ROOT, k + 1 : k + 9, :])
    for k in souths:
        root = jnp.abs(factors[ROOT, k : k + 8, :])
        factors[SOUTH, k : k + 8, :] = ts[k : k + 8, :] * root * pltpu.roll(root, 127, 1)


def spread(values, lane):
    return jnp.broadcast_to(values[:, lane : lane + 1], (8, 128))


def set_factors(coef, row, places, factors, lane):
    for which, c in places:
        value = spread(factors[which, c : c + 8, :], lane)
        coef[which, row, c : c + 8, :] = jnp.abs(value) if which == ROOT else value
    return value


def to_source(s, row, c, signed):
    root = jnp.abs(signed)
    supply = jnp.where(signed < 0.0, PAD_GAIN, 0.0)
    for half in range(2):
        s[half, row, pl.ds(c, 8), :] = (supply - s[half, row, pl.ds(c, 8), :]) * root


def all_at(c):
    return [(EAST, c), (SOUTH, c), (ROOT, c)]


def neighbours(src, coef, base, count, c, emit):
    above = [src[half, base - 1, pl.ds(c, 8), :] for half in range(2)]
    here = [src[half, base, pl.ds(c, 8), :] for half in range(2)]
    north = coef[SOUTH, base - 1, pl.ds(c, 8), :]
    for step in range(count):
        row = base + step
        east = coef[EAST, row, pl.ds(c, 8), :]
        west = coef[EAST, row, pl.ds(c - 1, 8), :]
        south = coef[SOUTH, row, pl.ds(c, 8), :]
        for half in range(2):
            below = src[half, row + 1, pl.ds(c, 8), :]
            total = east * src[half, row, pl.ds(c + 1, 8), :] + west * src[half, row, pl.ds(c - 1, 8), :]
            total = total + (south * below + north * above[half])
            emit(half, row, c, total, here[half])
            above[half], here[half] = here[half], below
        north = south


def sweep(src, coef, first, last, columns, unroll, emit):
    full = (last - first) // unroll
    for c in columns:
        if full == 1:
            neighbours(src, coef, first, unroll, c, emit)
        elif full > 1:

            def trip(index, carry, c=c):
                neighbours(src, coef, first + index * unroll, unroll, c, emit)
                return carry

            lax.fori_loop(0, full, trip, 0)
        if first + full * unroll < last:
            neighbours(src, coef, first + full * unroll, last - first - full * unroll, c, emit)


def adding(target):
    def emit(half, row, c, total, here):
        target[half, row, pl.ds(c, 8), :] = here + total

    return emit


def placing(target):
    def emit(half, row, c, total, here):
        target[half, row, pl.ds(c, 8), :] = total

    return emit


def result(s, u, coef, half, row, c, total):
    value = s[half, row, pl.ds(c, 8), :] + (MIX * u[half, row, pl.ds(c, 8), :] + TOP * total)
    return value * coef[ROOT, row, pl.ds(c, 8), :]


def corner_cells():
    for half in range(2):
        for side in range(2):
            for distance in (1, 2, 3):
                yield (half * 2 + side) * 6 + (0, 3, 5)[distance - 1], half, side, distance


def pack_kernel(*refs):
    small, load = refs[:5], refs[5]
    to_right, to_left, to_down, to_up, tiny_down, tiny_up, te, ts, tx = refs[6:15]
    edge, sem_edge, sem_rows, sem_small = refs[20:]
    table, east_class, south_class, leakage, pad_mask = refs[15:20]
    edges, tops = [], []
    nodes = [pltpu.make_async_copy(source, target, sem_small.at[i]) for i, (source, target) in enumerate(zip(small, refs[15:20]))]
    for copy in nodes:
        copy.start()
    for side in range(2):
        for half in range(2):
            copy = pltpu.make_async_copy(
                load.at[:, pl.ds(side * (SIDE - 8), 8), pl.ds(half * 128, 128)], edge.at[side, half], sem_edge.at[side, half]
            )
            copy.start()
            edges.append(copy)
    for side, message in enumerate((to_up, to_down)):
        for half in range(2):
            for row in range(4):
                copy = pltpu.make_async_copy(
                    load.at[side * (SIDE - 4) + row, :, pl.ds(half * 128, 128)],
                    message.at[pl.ds((half * 4 + row) * SIDE, SIDE), :],
                    sem_rows.at[side, half, row],
                )
                copy.start()
                tops.append(copy)

    for copy in nodes:
        copy.wait()

    def look_up(classes):
        found = jnp.zeros((SIDE, SIDE), F32)
        for label in range(8):
            found = jnp.where(classes == label, table[label], found)
        return found

    zeros = jnp.zeros((SIDE, 128 - SIDE), F32)

    def turned(values):
        return pltpu.roll(jnp.concatenate([values.T, zeros], axis=1), 8, 1)

    east = turned(look_up(east_class[...]))
    south = turned(look_up(south_class[...]))
    ground = turned(leakage[...] + PAD_GAIN * pad_mask[...].astype(F32))
    for target, values in ((te, east), (ts, south), (tx, ground)):
        target[0:8, :] = jnp.zeros((8, 128), F32)
        target[8 : SIDE + 8, :] = values
        target[SIDE + 8 :, :] = jnp.zeros((16, 128), F32)
    lane = lanes_of((SIDE, 128))

    def banded(shifts):
        first, second, third = [
            values if shift == 0 else pltpu.roll(values, shift, 1) for values, shift in zip((east, south, ground), shifts)
        ]
        return jnp.where(lane < 8, first, jnp.where(lane < 16, second, third))

    tiny_down[0:SIDE, :] = banded((64, 72, 80))
    tiny_up[0:SIDE, :] = banded((120, 0, 8))
    for copy in edges:
        copy.wait()
    for offset, half, side, distance in corner_cells():
        count = 4 - distance
        at = SIDE + offset
        columns = slice(8 - count, 8) if side else slice(0, count)
        tiny_down[at : at + count, :] = edge[side, half, SIDE - distance, columns, :]
        tiny_up[at : at + count, :] = edge[side, half, distance - 1, columns, :]
    for side, message in enumerate((to_left, to_right)):
        for half in range(2):
            for row in range(SIDE):
                base = (half * SIDE + row) * 4
                message[base : base + 4, :] = edge[side, half, row, side * 4 : side * 4 + 4, :]
    for copy in tops:
        copy.wait()


def put_conductances(message, base, te, ts, tx, first_east, first_other):
    message[base : base + 5, :] = te[first_east : first_east + 5, :]
    message[base + 5 : base + 9, :] = ts[first_other : first_other + 4, :]
    message[base + 9 : base + 13, :] = tx[first_other : first_other + 4, :]
    message[base + 13 : base + 16, :] = jnp.zeros((3, 128), F32)


def first_kernel(te, ts, tx, load, s, x1, coef, factors, sem):
    def part(group, half):
        return pltpu.make_async_copy(
            load.at[pl.ds(group * 8, 8), :, pl.ds(half * 128, 128)],
            s.at[half, pl.ds(4 + group * 8, 8), pl.ds(8, SIDE), :],
            sem.at[group, half],
        )

    for group in range(SIDE // 8):
        for half in range(2):
            part(group, half).start()
    own = range(8, SIDE + 8, 8)
    turn_factors(te, ts, tx, factors, own, own, own)

    def body(group, carry):
        for half in range(2):
            part(group, half).wait()
        for step in range(8):
            row = group * 8 + 4 + step
            for c in own:
                to_source(s, row, c, set_factors(coef, row, all_at(c), factors, 8 + step))
        for c in own:
            neighbours(s, coef, group * 8 + 3, 8, c, adding(x1))
            for which in range(3):
                factors[which, c : c + 8, :] = pltpu.roll(factors[which, c : c + 8, :], 120, 1)
        return carry

    lax.fori_loop(0, SIDE // 8, body, 0)


def corner_kernel(te, ts, tx, from_up, from_down, right, left, to_right, to_left, te2, ts2, tx2):
    lane = lanes_of((SIDE, 128))
    upper, lower = from_up[0:SIDE, :], from_down[0:SIDE, :]
    for source, target, down, up in ((te, te2, 0, 72), (ts, ts2, 120, 64), (tx, tx2, 112, 56)):
        head = pltpu.roll(upper, down, 1) if down else upper
        tail = pltpu.roll(lower, up, 1)
        own = source[8 : SIDE + 8, :]
        target[0:8, :] = jnp.zeros((8, 128), F32)
        target[8 : SIDE + 8, :] = jnp.where(lane < 8, head, jnp.where(lane < SIDE + 8, own, tail))
        target[SIDE + 8 :, :] = jnp.zeros((16, 128), F32)
    to_right[0:MAIN_MSG, :] = right[...]
    to_left[0:MAIN_MSG, :] = left[...]
    for offset, half, below, distance in corner_cells():
        count = 4 - distance
        origin = from_down if below else from_up
        for side, message in enumerate((to_left, to_right)):
            at = SIDE + (half * 2 + side) * 6 + (0, 3, 5)[distance - 1]
            message[MAIN_MSG + offset : MAIN_MSG + offset + count, :] = origin[at : at + count, :]
    put_conductances(to_right, MAIN_MSG + 24, te2, ts2, tx2, SIDE + 3, SIDE + 4)
    put_conductances(to_left, MAIN_MSG + 24, te2, ts2, tx2, 8, 8)


def main_kernel(te, ts, tx, from_up, from_down, own_up, *rest):
    s, x1, coef, u, t, done, factors = rest[3:]
    own = range(8, SIDE + 8, 8)
    turn_factors(te, ts, tx, factors, own, own, own)
    for half in range(2):
        for row in range(4):
            at = (half * 4 + row) * SIDE
            s[half, row, 8 : SIDE + 8, :] = from_up[at : at + SIDE, :]
            s[half, SIDE + 4 + row, 8 : SIDE + 8, :] = from_down[at : at + SIDE, :]
        s[half, 4, 8 : SIDE + 8, :] = own_up[half * 4 * SIDE : half * 4 * SIDE + SIDE, :]
    for row in (0, 1, 2, 3, 4, SIDE + 3, SIDE + 4, SIDE + 5, SIDE + 6, SIDE + 7):
        for c in own:
            signed = set_factors(coef, row, all_at(c), factors, row + 4)
            if row != SIDE + 3:
                to_source(s, row, c, signed)
    sweep(s, coef, 1, 6, own, 5, adding(x1))
    sweep(s, coef, SIDE + 3, SIDE + 7, own, 4, adding(x1))
    sweep(x1, coef, 2, SIDE + 6, own, 17, placing(u))
    sweep(u, coef, 3, SIDE + 5, own, 22, placing(t))

    def finish(half, row, c, total, here):
        done[half, row - 4, c - 8 : c, :] = result(s, u, coef, half, row, c, total)

    sweep(t, coef, 4, SIDE + 4, range(16, SIDE, 8), 16, finish)


def side_kernel(side, *refs):
    te2, ts2, tx2, message = refs[:4]
    s, x1, coef, u, t, out, done, te, ts, tx, factors, sem = refs[-12:]
    ready = refs[4 if side else 7]
    first, width = (8, SIDE - 16) if side else (SIDE - 8, 8)
    outs = []
    for half in range(2):
        copy = pltpu.make_async_copy(
            ready.at[half, :, pl.ds(8, width), :] if side else ready.at[half],
            out.at[:, pl.ds(first, width), pl.ds(half * 128, 128)],
            sem.at[2, half],
        )
        copy.start()
        outs.append(copy)
    for source, target in ((te2, te), (ts2, ts), (tx2, tx)):
        target[...] = source[...]
    at = MAIN_MSG + 24
    first_east, first_other = (SIDE + 8, SIDE + 8) if side else (3, 4)
    te[first_east : first_east + 5, :] = message[at : at + 5, :]
    ts[first_other : first_other + 4, :] = message[at + 5 : at + 9, :]
    tx[first_other : first_other + 4, :] = message[at + 9 : at + 13, :]
    c = SIDE + 8 if side else 1
    places = [(EAST, SIDE + 7 if side else 1), (SOUTH, c), (ROOT, c)]
    turn_factors(te, ts, tx, factors, (SIDE, c) if side else (c, 8), (places[0][1],), (c,))
    halo = SIDE + 8 if side else 4
    for row in range(SIDE):
        for half in range(2):
            at = (half * SIDE + row) * 4
            s[half, row + 4, halo : halo + 4, :] = message[at : at + 4, :]
            if side == 0:
                s[half, row + 4, 8:9, :] = refs[4][at : at + 1, :]
    if side == 0:
        for half in range(2):
            for row in range(4):
                at = (half * 4 + row) * SIDE
                s[half, row, 8:9, :] = refs[5][at : at + 1, :]
                s[half, SIDE + 4 + row, 8:9, :] = refs[6][at : at + 1, :]
    for offset, half, below, distance in corner_cells():
        count = 4 - distance
        row = SIDE + 3 + distance if below else 4 - distance
        start = SIDE + 8 if side else 8 - count
        s[half, row, start : start + count, :] = message[MAIN_MSG + offset : MAIN_MSG + offset + count, :]

    def body(group, carry):
        for step in range(8):
            row = group * 8 + step
            to_source(s, row, c, set_factors(coef, row, places, factors, 4 + step))
        for which, k in places:
            factors[which, k : k + 8, :] = pltpu.roll(factors[which, k : k + 8, :], 120, 1)
        return carry

    lax.fori_loop(0, ROWS // 8, body, 0)
    sweep(s, coef, 1, SIDE + 7, (SIDE + 4 if side else 4,), 14, adding(x1))
    sweep(x1, coef, 2, SIDE + 6, (SIDE + 3 if side else 5,), 17, placing(u))
    sweep(u, coef, 3, SIDE + 5, (SIDE + 2 if side else 6,), 22, placing(t))

    def finish(half, row, c, total, here):
        done[half, row - 4, :, :] = result(s, u, coef, half, row, c, total)

    for part in range(2):
        rows = pl.ds(part * (SIDE // 2), SIDE // 2)
        sweep(t, coef, 4 + part * (SIDE // 2), 4 + (part + 1) * (SIDE // 2), (SIDE if side else 8,), 16, finish)
        for half in range(2):
            if side == 0:
                copy = pltpu.make_async_copy(
                    done.at[half, rows],
                    out.at[rows, pl.ds(0, 8), pl.ds(half * 128, 128)],
                    sem.at[part, half],
                )
                copy.start()
                outs.append(copy)
    for copy in outs:
        copy.wait()


VMEM = pl.BlockSpec(memory_space=pltpu.VMEM)
HBM = pl.BlockSpec(memory_space=pltpu.HBM)
DMA = pltpu.SemaphoreType.DMA
FIELD = pltpu.VMEM((2, ROWS, COLS, 128), F32)
COEF = pltpu.VMEM((3, ROWS, COLS, 128), F32)
TURNED = pltpu.VMEM((TURNED_ROWS, 128), F32)
FACTORS = pltpu.VMEM((3, TURNED_ROWS, 128), F32)


def call(kernel, in_specs, out_shape, out_specs, scratch, cost, grant, aliases=None):
    return pl.pallas_call(
        kernel,
        in_specs=in_specs,
        out_shape=out_shape,
        out_specs=out_specs,
        scratch_shapes=scratch,
        input_output_aliases=aliases or {},
        cost_estimate=pl.CostEstimate(flops=cost, bytes_accessed=1 << 20, transcendentals=0),
        compiler_params=pltpu.CompilerParams(vmem_limit_bytes=grant << 20),
    )


def block(east_class, south_class, cond_table, leakage, pad_mask, load):
    gx, gy = lax.axis_size("gx"), lax.axis_size("gy")

    def shift(values, axis, step):
        count = gx if axis == "gx" else gy
        return lax.ppermute(values, axis, [(i, (i + step) % count) for i in range(count)])

    potential = pltpu.HBM((SIDE, SIDE, 256), F32)
    given = [pltpu.with_memory_space_constraint(a, pltpu.HBM) for a in (cond_table, east_class, south_class, leakage, pad_mask, load)]
    right, left, to_down, to_up, tiny_down, tiny_up, te, ts, tx = call(
        pack_kernel,
        [HBM] * 6,
        [pltpu.VMEM((MAIN_MSG, 128), F32)] * 4 + [pltpu.VMEM((TINY_MSG, 128), F32)] * 2 + [TURNED] * 3,
        [VMEM] * 9,
        [pltpu.SMEM((8,), F32)]
        + [pltpu.VMEM((SIDE, SIDE), kind) for kind in (jnp.int32, jnp.int32, F32, jnp.int32)]
        + [pltpu.VMEM((2, 2, SIDE, 8, 128), F32), DMA((2, 2)), DMA((2, 2, 4)), DMA((5,))],
        1 << 22,
        4,
    )(*given)
    tiny_from_up = shift(tiny_down, "gx", 1)
    tiny_from_down = shift(tiny_up, "gx", -1)
    from_up = shift(to_down, "gx", 1)
    from_down = shift(to_up, "gx", -1)
    to_right, to_left, te2, ts2, tx2 = call(
        corner_kernel, [VMEM] * 7, [pltpu.VMEM((FULL_MSG, 128), F32)] * 2 + [TURNED] * 3, [VMEM] * 5, [], 1 << 20, 4
    )(te, ts, tx, tiny_from_up, tiny_from_down, right, left)
    from_left = shift(to_right, "gy", 1)
    from_right = shift(to_left, "gy", -1)
    s, x1, coef = call(
        first_kernel, [VMEM] * 3 + [HBM], [FIELD, FIELD, COEF], [VMEM] * 3, [FACTORS, DMA((SIDE // 8, 2))], 1 << 25, 4
    )(te, ts, tx, given[5])
    *state, middle = call(
        main_kernel,
        [VMEM] * 9,
        [FIELD, FIELD, COEF, FIELD, FIELD, pltpu.VMEM((2, SIDE, SIDE, 128), F32)],
        [VMEM] * 6,
        [FACTORS],
        1 << 25,
        4,
        {6 + i: i for i in range(3)},
    )(te2, ts2, tx2, from_up, from_down, to_up, s, x1, coef)
    strip = pltpu.VMEM((2, SIDE, 8, 128), F32)
    *state, out, right_strip = call(
        functools.partial(side_kernel, 1),
        [VMEM] * 10,
        [FIELD, FIELD, COEF, FIELD, FIELD, potential, strip],
        [VMEM] * 5 + [HBM, VMEM],
        [TURNED] * 3 + [FACTORS, DMA((3, 2))],
        1 << 23,
        4,
        {5 + i: i for i in range(5)},
    )(te2, ts2, tx2, from_right, middle, *state)
    *state, out = call(
        functools.partial(side_kernel, 0),
        [VMEM] * 13 + [HBM],
        [FIELD, FIELD, COEF, FIELD, FIELD, potential],
        [VMEM] * 5 + [HBM],
        [strip] + [TURNED] * 3 + [FACTORS, DMA((3, 2))],
        1 << 23,
        4,
        {8 + i: i for i in range(6)},
    )(te2, ts2, tx2, from_left, left, from_up, from_down, right_strip, *state, out)
    return out


def solution(mesh):
    in_specs = (P("gx", "gy"), P("gx", "gy"), P(), P("gx", "gy"), P("gx", "gy"), P("gx", "gy", None))
    return jax.shard_map(block, mesh=mesh, in_specs=in_specs, out_specs=P("gx", "gy", None), check_vma=False)
```

time: 37.4 us -> 36.4 us (0.973)
  starting transfers between devices: 18.8 us -> 10.4 us
  waiting for transfers between devices: 1.82 us -> 9.1 us
    ppermute x6, starting transfers between devices: 18.8 us -> 10.4 us  [shift(): lax.ppermute(values, axis, [(i, (i + step) % count) for i in range(count)])]
    ppermute x6, waiting for transfers between devices: 1.82 us -> 9.1 us  [shift(): lax.ppermute(values, axis, [(i, (i + step) % count) for i in range(count)])]
    pallas_call x4 -> x5, Pallas kernels: 12.2 us -> 12.5 us  [the longest x1 5.45 us: block(): call(main_kernel, [VMEM] * 9, [FIELD, FIELD, COEF, FIELD, FIELD, pltpu.VM...]
  transfers between devices with their start and end apart: 6 -> 6, of which waited for: 1 -> 3; matrix products, arithmetic and copies ran while one was open for 0% -> 0% of each run, Pallas kernels for 28% -> 33%
where the time goes in v3:
time: 36.4 us; the launch traced here: 36.3 us
  Pallas kernels  16.7 us (46%)
  starting transfers between devices  10.4 us (29%)
  waiting for transfers between devices  9.1 us (25%)
    ppermute x6, starting transfers between devices, shift(): lax.ppermute(values, axis, [(i, (i + step) % count) for i in range(count)])  10.4 us
    ppermute x6, waiting for transfers between devices, shift(): lax.ppermute(values, axis, [(i, (i + step) % count) for i in range(count)])  9.1 us
    pallas_call x1, Pallas kernels, block(): call(main_kernel, [VMEM] * 9, [FIELD, FIELD, COEF, FIELD, FIELD, pltpu.VM...  5.45 us
    pallas_call x1, Pallas kernels, block(): call(first_kernel, [VMEM] * 3 + [HBM], [FIELD, FIELD, COEF], [VMEM] * 3,...  4.21 us
    pallas_call x1, Pallas kernels, block(): call(functools.partial(side_kernel, 0), [VMEM] * 13 + [HBM], [FIELD, FIEL...  2.85 us
    pallas_call x1, Pallas kernels, block(): call(functools.partial(side_kernel, 1), [VMEM] * 10, [FIELD, FIELD, COEF,...  2.2 us
    pallas_call x1, Pallas kernels, block(): call(pack_kernel, [HBM] * 6, [pltpu.VMEM((MAIN_MSG, 128), F32)] * 4 + [pl...  1.88 us
  transfers between devices with their start and end apart: 6, of which 3 were waited for; matrix products, arithmetic and copies ran while one was open for 0% of the time, Pallas kernels for 33%

profile of v3, /device:TPU:7, one launch (start us, length us, event | category | flops | bytes accessed | tf_op | source)
XLA Modules:
  0.0 36.3 jit_solution(18130221240114892006)
XLA Ops:
  0.0 1.9 %shard_map.64 = (f32[512,128]{1,0:T(8,128)S(1)}, f32[512,128]{1,0:T(8,128)S(1)}, f32[512,128]{1,0:T(8,128)S(1)}, f32[512,128]{1,0:T(8,128)S(1)}, f32[88,128]{1,0...) custom-call(f32[8]{0:T(128)} %refs_0_.1, ...), custom_call_target="tpu_custom_call" | custom-call | flops 4194304 | bytes 1048576 | tf_op jit(solution)/shard_map/pallas_call | solution.py:407
  1.9 1.8 %collective-permute-start = (f32[88,128]{1,0:T(8,128)S(1)}, f32[88,128]{1,0:T(8,128)S(1)}, u32[]{:S(2)}, u32[]{:S(2)}) collective-permute-start(f32[88,128]{1,0:T(8,128)S(1)} %get-tuple-element.39), channel_id=1, source_target_pairs={{0,16},{16,32},{32,48},{48,64},{64,80},{80,96},{96,112},{112,128},... | collective-permute-start | bytes 135176 | tf_op jit(solution)/shard_map/ppermute | solution.py:403
  3.7 0.0 collective-permute-start.1
  3.7 1.1 %collective-permute-done.from_up = f32[88,128]{1,0:T(8,128)S(1)} collective-permute-done((f32[88,128]{1,0:T(8,128)S(1)}, f32[88,128]{1,0:T(8,128)S(1)}, u32[]{:S(2)}, u32[]{:S(2)}) %collective-permute-start) | collective-permute-done | bytes 45088 | tf_op jit(solution)/shard_map/ppermute | solution.py:403
  4.9 4.4 %collective-permute-done.1.from_down = f32[88,128]{1,0:T(8,128)S(1)} collective-permute-done((f32[88,128]{1,0:T(8,128)S(1)}, f32[88,128]{1,0:T(8,128)S(1)}, u32[]{:S(2)}, u32[]{:S(2)}) %collective-permute-start.1) | collective-permute-done | bytes 45088 | tf_op jit(solution)/shard_map/ppermute | solution.py:403
  9.3 0.1 shard_map.65
  9.5 8.0 %collective-permute-start.5 = (f32[552,128]{1,0:T(8,128)S(1)}, f32[552,128]{1,0:T(8,128)S(1)}, u32[]{:S(2)}, u32[]{:S(2)}) collective-permute-start(f32[552,128]{1,0:T(8,128)S(1)} %get-tuple-element.49), channel_id=1, source_target_pairs={{0,15},{1,0},{2,1},{3,2},{4,3},{5,4},{6,5},{7,6},{8,7},{9,8},{10,9... | collective-permute-start | bytes 847880 | tf_op jit(solution)/shard_map/ppermute | solution.py:403
  17.5 0.0 collective-permute-start.2
  17.5 0.0 collective-permute-start.3
  17.5 0.5 %collective-permute-start.4 = (f32[512,128]{1,0:T(8,128)S(1)}, f32[512,128]{1,0:T(8,128)S(1)}, u32[]{:S(2)}, u32[]{:S(2)}) collective-permute-start(f32[512,128]{1,0:T(8,128)S(1)} %get-tuple-element.48.own_up), channel_id=1, source_target_pairs={{0,240},{16,0},{32,16},{48,32},{64,48},{80,64},{96,80},{112,96},{1... | collective-permute-start | bytes 786440 | tf_op jit(solution)/shard_map/ppermute | solution.py:403
  18.0 4.2 %shard_map.66 = (f32[2,72,80,128]{3,2,1,0:T(8,128)S(1)}, f32[2,72,80,128]{3,2,1,0:T(8,128)S(1)}, f32[3,72,80,128]{3,2,1,0:T(8,128)S(1)}) custom-call(f32[88,128]{1,0:T(8,128)S(1)} %get-tuple-element.36.te, f32[88,128]{1,0:T(8,128)S(1)} %get-tuple-element.37.ts, f32[88,128]{1,0:T(8,128)S(1)} %get-tuple-element.38.tx, f32[64,64,256]{2,1,0:T(8,128)} %load.1), custom_call_target="tpu_custom_call" | custom-call | flops 33554432 | bytes 1048576 | tf_op jit(solution)/shard_map/pallas_call | solution.py:427
  22.2 0.0 collective-permute-done.3.from_up.refs_5_
  22.2 3.5 %collective-permute-done.4.from_down.refs_6_ = f32[512,128]{1,0:T(8,128)S(1)} collective-permute-done((f32[512,128]{1,0:T(8,128)S(1)}, f32[512,128]{1,0:T(8,128)S(1)}, u32[]{:S(2)}, u32[]{:S(2)}) %collective-permute-start.4) | collective-permute-done | bytes 262176 | tf_op jit(solution)/shard_map/ppermute | solution.py:403
  25.7 5.4 %shard_map.67 = (f32[2,72,80,128]{3,2,1,0:T(8,128)S(1)}, f32[2,72,80,128]{3,2,1,0:T(8,128)S(1)}, f32[3,72,80,128]{3,2,1,0:T(8,128)S(1)}, f32[2,72,80,128]{3,2,1,...) custom-call(f32[88,128]{1,0:T(8,128)S(1)} %get-tuple-element.43.te.r, ...), custom_call_target="tpu_custom_call", output_to_operand_aliasing={{0}: (6, {}), {1}: (7, {}), {2}: (8, {})} | custom-call | flops 33554432 | bytes 1048576 | tf_op jit(solution)/shard_map/pallas_call | solution.py:430
  31.2 0.0 collective-permute-done.5.refs_3_
  31.2 2.2 %shard_map.68 = (f32[2,72,80,128]{3,2,1,0:T(8,128)S(1)}, f32[2,72,80,128]{3,2,1,0:T(8,128)S(1)}, f32[3,72,80,128]{3,2,1,0:T(8,128)S(1)}, f32[2,72,80,128]{3,2,1,...) custom-call(f32[88,128]{1,0:T(8,128)S(1)} %get-tuple-element.43.te.r, ...), custom_call_target="tpu_custom_call", output_to_operand_aliasing={{0}: (5, {}), {1}: (6, {}), {2}: (7, {}), {3}: (8, {}), {4}... | custom-call | flops 8388608 | bytes 1048576 | tf_op jit(solution)/shard_map/pallas_call | solution.py:441
  33.4 0.0 collective-permute-done.2.refs_3_
  33.4 2.9 %shard_map.69 = (f32[2,72,80,128]{3,2,1,0:T(8,128)S(1)}, f32[2,72,80,128]{3,2,1,0:T(8,128)S(1)}, f32[3,72,80,128]{3,2,1,0:T(8,128)S(1)}, f32[2,72,80,128]{3,2,1,...) custom-call(f32[88,128]{1,0:T(8,128)S(1)} %get-tuple-element.43.te.r, ...), custom_call_target="tpu_custom_call", output_to_operand_aliasing={{0}: (8, {}), {1}: (9, {}), {2}: (10, {}), {3}: (11, {}), {... | custom-call | flops 8388608 | bytes 1048576 | tf_op jit(solution)/shard_map/pallas_call | solution.py:451
Async XLA Ops:
  1.9 3.0 %collective-permute-start = (f32[88,128]{1,0:T(8,128)S(1)}, f32[88,128]{1,0:T(8,128)S(1)}, u32[]{:S(2)}, u32[]{:S(2)}) collective-permute-start(f32[88,128]{1,0:T(8,128)S(1)} %get-tuple-element.39), channel_id=1, source_target_pairs={{0,16},{16,32},{32,48},{48,64},{64,80},{80,96},{96,112},{112,128},... | collective-permute-start | bytes 135176 | tf_op jit(solution)/shard_map/ppermute | solution.py:403
  3.7 5.6 %collective-permute-start.1 = (f32[88,128]{1,0:T(8,128)S(1)}, f32[88,128]{1,0:T(8,128)S(1)}, u32[]{:S(2)}, u32[]{:S(2)}) collective-permute-start(f32[88,128]{1,0:T(8,128)S(1)} %get-tuple-element.40), channel_id=1, source_target_pairs={{0,240},{16,0},{32,16},{48,32},{64,48},{80,64},{96,80},{112,96},{1... | collective-permute-start | bytes 135176 | tf_op jit(solution)/shard_map/ppermute | solution.py:403
  9.5 21.7 %collective-permute-start.5 = (f32[552,128]{1,0:T(8,128)S(1)}, f32[552,128]{1,0:T(8,128)S(1)}, u32[]{:S(2)}, u32[]{:S(2)}) collective-permute-start(f32[552,128]{1,0:T(8,128)S(1)} %get-tuple-element.49), channel_id=1, source_target_pairs={{0,15},{1,0},{2,1},{3,2},{4,3},{5,4},{6,5},{7,6},{8,7},{9,8},{10,9... | collective-permute-start | bytes 847880 | tf_op jit(solution)/shard_map/ppermute | solution.py:403
  17.5 15.9 %collective-permute-start.2 = (f32[552,128]{1,0:T(8,128)S(1)}, f32[552,128]{1,0:T(8,128)S(1)}, u32[]{:S(2)}, u32[]{:S(2)}) collective-permute-start(f32[552,128]{1,0:T(8,128)S(1)} %get-tuple-element.46), channel_id=1, source_target_pairs={{0,1},{1,2},{2,3},{3,4},{4,5},{5,6},{6,7},{7,8},{8,9},{9,10},{10,1... | collective-permute-start | bytes 847880 | tf_op jit(solution)/shard_map/ppermute | solution.py:403
  17.5 4.7 %collective-permute-start.3 = (f32[512,128]{1,0:T(8,128)S(1)}, f32[512,128]{1,0:T(8,128)S(1)}, u32[]{:S(2)}, u32[]{:S(2)}) collective-permute-start(f32[512,128]{1,0:T(8,128)S(1)} %get-tuple-element.47), channel_id=1, source_target_pairs={{0,16},{16,32},{32,48},{48,64},{64,80},{80,96},{96,112},{112,128},... | collective-permute-start | bytes 786440 | tf_op jit(solution)/shard_map/ppermute | solution.py:403
  17.5 8.2 %collective-permute-start.4 = (f32[512,128]{1,0:T(8,128)S(1)}, f32[512,128]{1,0:T(8,128)S(1)}, u32[]{:S(2)}, u32[]{:S(2)}) collective-permute-start(f32[512,128]{1,0:T(8,128)S(1)} %get-tuple-element.48.own_up), channel_id=1, source_target_pairs={{0,240},{16,0},{32,16},{48,32},{64,48},{80,64},{96,80},{112,96},{1... | collective-permute-start | bytes 786440 | tf_op jit(solution)/shard_map/ppermute | solution.py:403

commit v4 on v3

--- a/solution.py
+++ b/solution.py
@@ -131,6 +131,10 @@
     return value * coef[ROOT, row, pl.ds(c, 8), :]
 
 
+def even_row():
+    return lax.rem(lax.axis_index("gx"), 2) == 0
+
+
 def corner_cells():
     for half in range(2):
         for side in range(2):
@@ -140,7 +144,9 @@
 
 def pack_kernel(*refs):
     small, load = refs[:5], refs[5]
-    to_right, to_left, to_down, to_up, tiny_down, tiny_up, te, ts, tx = refs[6:15]
+    to_right, to_left, to_near, to_far, tiny_near, tiny_far, te, ts, tx = refs[6:15]
+    even = even_row()
+    near, far = jnp.where(even, SIDE - 4, 0), jnp.where(even, 0, SIDE - 4)
     edge, sem_edge, sem_rows, sem_small = refs[20:]
     table, east_class, south_class, leakage, pad_mask = refs[15:20]
     edges, tops = [], []
@@ -154,13 +160,13 @@
             )
             copy.start()
             edges.append(copy)
-    for side, message in enumerate((to_up, to_down)):
+    for place, (start, message) in enumerate(((near, to_near), (far, to_far))):
         for half in range(2):
             for row in range(4):
                 copy = pltpu.make_async_copy(
-                    load.at[side * (SIDE - 4) + row, :, pl.ds(half * 128, 128)],
+                    load.at[start + row, :, pl.ds(half * 128, 128)],
                     message.at[pl.ds((half * 4 + row) * SIDE, SIDE), :],
-                    sem_rows.at[side, half, row],
+                    sem_rows.at[place, half, row],
                 )
                 copy.start()
                 tops.append(copy)
@@ -194,16 +200,17 @@
         ]
         return jnp.where(lane < 8, first, jnp.where(lane < 16, second, third))
 
-    tiny_down[0:SIDE, :] = banded((64, 72, 80))
-    tiny_up[0:SIDE, :] = banded((120, 0, 8))
+    lower, upper = banded((64, 72, 80)), banded((120, 0, 8))
+    tiny_near[0:SIDE, :] = jnp.where(even, lower, upper)
+    tiny_far[0:SIDE, :] = jnp.where(even, upper, lower)
     for copy in edges:
         copy.wait()
     for offset, half, side, distance in corner_cells():
         count = 4 - distance
         at = SIDE + offset
         columns = slice(8 - count, 8) if side else slice(0, count)
-        tiny_down[at : at + count, :] = edge[side, half, SIDE - distance, columns, :]
-        tiny_up[at : at + count, :] = edge[side, half, distance - 1, columns, :]
+        tiny_near[at : at + count, :] = edge[side, half, jnp.where(even, SIDE - distance, distance - 1), columns, :]
+        tiny_far[at : at + count, :] = edge[side, half, jnp.where(even, distance - 1, SIDE - distance), columns, :]
     for side, message in enumerate((to_left, to_right)):
         for half in range(2):
             for row in range(SIDE):
@@ -250,9 +257,11 @@
     lax.fori_loop(0, SIDE // 8, body, 0)
 
 
-def corner_kernel(te, ts, tx, from_up, from_down, right, left, to_right, to_left, te2, ts2, tx2):
+def corner_kernel(te, ts, tx, near, far, right, left, to_right, to_left, te2, ts2, tx2):
     lane = lanes_of((SIDE, 128))
-    upper, lower = from_up[0:SIDE, :], from_down[0:SIDE, :]
+    even = even_row()
+    upper = jnp.where(even, far[0:SIDE, :], near[0:SIDE, :])
+    lower = jnp.where(even, near[0:SIDE, :], far[0:SIDE, :])
     for source, target, down, up in ((te, te2, 0, 72), (ts, ts2, 120, 64), (tx, tx2, 112, 56)):
         head = pltpu.roll(upper, down, 1) if down else upper
         tail = pltpu.roll(lower, up, 1)
@@ -264,24 +273,29 @@
     to_left[0:MAIN_MSG, :] = left[...]
     for offset, half, below, distance in corner_cells():
         count = 4 - distance
-        origin = from_down if below else from_up
         for side, message in enumerate((to_left, to_right)):
             at = SIDE + (half * 2 + side) * 6 + (0, 3, 5)[distance - 1]
-            message[MAIN_MSG + offset : MAIN_MSG + offset + count, :] = origin[at : at + count, :]
+            first, second = (near, far) if below else (far, near)
+            message[MAIN_MSG + offset : MAIN_MSG + offset + count, :] = jnp.where(
+                even, first[at : at + count, :], second[at : at + count, :]
+            )
     put_conductances(to_right, MAIN_MSG + 24, te2, ts2, tx2, SIDE + 3, SIDE + 4)
     put_conductances(to_left, MAIN_MSG + 24, te2, ts2, tx2, 8, 8)
 
 
-def main_kernel(te, ts, tx, from_up, from_down, own_up, *rest):
-    s, x1, coef, u, t, done, factors = rest[3:]
+def main_kernel(te, ts, tx, near, far, own_near, own_far, *rest):
+    s, x1, coef, u, t, out, factors, done, sem = rest[3:]
+    even = even_row()
     own = range(8, SIDE + 8, 8)
     turn_factors(te, ts, tx, factors, own, own, own)
     for half in range(2):
         for row in range(4):
             at = (half * 4 + row) * SIDE
-            s[half, row, 8 : SIDE + 8, :] = from_up[at : at + SIDE, :]
-            s[half, SIDE + 4 + row, 8 : SIDE + 8, :] = from_down[at : at + SIDE, :]
-        s[half, 4, 8 : SIDE + 8, :] = own_up[half * 4 * SIDE : half * 4 * SIDE + SIDE, :]
+            one, other = near[at : at + SIDE, :], far[at : at + SIDE, :]
+            s[half, row, 8 : SIDE + 8, :] = jnp.where(even, other, one)
+            s[half, SIDE + 4 + row, 8 : SIDE + 8, :] = jnp.where(even, one, other)
+        at = half * 4 * SIDE
+        s[half, 4, 8 : SIDE + 8, :] = jnp.where(even, own_far[at : at + SIDE, :], own_near[at : at + SIDE, :])
     for row in (0, 1, 2, 3, 4, SIDE + 3, SIDE + 4, SIDE + 5, SIDE + 6, SIDE + 7):
         for c in own:
             signed = set_factors(coef, row, all_at(c), factors, row + 4)
@@ -295,23 +309,36 @@
     def finish(half, row, c, total, here):
         done[half, row - 4, c - 8 : c, :] = result(s, u, coef, half, row, c, total)
 
-    sweep(t, coef, 4, SIDE + 4, range(16, SIDE, 8), 16, finish)
+    outs = []
+    for part in range(4):
+        rows = pl.ds(part * 16, 16)
+        sweep(t, coef, 4 + part * 16, 20 + part * 16, range(16, SIDE, 8), 16, finish)
+        for half in range(2):
+            copy = pltpu.make_async_copy(
+                done.at[half, rows, pl.ds(8, SIDE - 16), :],
+                out.at[rows, pl.ds(8, SIDE - 16), pl.ds(half * 128, 128)],
+                sem.at[part, half],
+            )
+            copy.start()
+            outs.append(copy)
+    for copy in outs:
+        copy.wait()
 
 
 def side_kernel(side, *refs):
     te2, ts2, tx2, message = refs[:4]
-    s, x1, coef, u, t, out, done, te, ts, tx, factors, sem = refs[-12:]
-    ready = refs[4 if side else 7]
-    first, width = (8, SIDE - 16) if side else (SIDE - 8, 8)
+    if side:
+        s, x1, coef, u, t, out, done, te, ts, tx, factors, sem = refs[-12:]
+    else:
+        s, x1, coef, u, t, done, te, ts, tx, factors = refs[-10:]
     outs = []
-    for half in range(2):
-        copy = pltpu.make_async_copy(
-            ready.at[half, :, pl.ds(8, width), :] if side else ready.at[half],
-            out.at[:, pl.ds(first, width), pl.ds(half * 128, 128)],
-            sem.at[2, half],
-        )
-        copy.start()
-        outs.append(copy)
+    if side:
+        for half in range(2):
+            copy = pltpu.make_async_copy(
+                refs[4].at[half], out.at[:, pl.ds(0, 8), pl.ds(half * 128, 128)], sem.at[2, half]
+            )
+            copy.start()
+            outs.append(copy)
     for source, target in ((te2, te), (ts2, ts), (tx2, tx)):
         target[...] = source[...]
     at = MAIN_MSG + 24
@@ -330,11 +357,13 @@
             if side == 0:
                 s[half, row + 4, 8:9, :] = refs[4][at : at + 1, :]
     if side == 0:
+        even = even_row()
         for half in range(2):
             for row in range(4):
                 at = (half * 4 + row) * SIDE
-                s[half, row, 8:9, :] = refs[5][at : at + 1, :]
-                s[half, SIDE + 4 + row, 8:9, :] = refs[6][at : at + 1, :]
+                one, other = refs[5][at : at + 1, :], refs[6][at : at + 1, :]
+                s[half, row, 8:9, :] = jnp.where(even, other, one)
+                s[half, SIDE + 4 + row, 8:9, :] = jnp.where(even, one, other)
     for offset, half, below, distance in corner_cells():
         count = 4 - distance
         row = SIDE + 3 + distance if below else 4 - distance
@@ -361,10 +390,10 @@
         rows = pl.ds(part * (SIDE // 2), SIDE // 2)
         sweep(t, coef, 4 + part * (SIDE // 2), 4 + (part + 1) * (SIDE // 2), (SIDE if side else 8,), 16, finish)
         for half in range(2):
-            if side == 0:
+            if side:
                 copy = pltpu.make_async_copy(
                     done.at[half, rows],
-                    out.at[rows, pl.ds(0, 8), pl.ds(half * 128, 128)],
+                    out.at[rows, pl.ds(SIDE - 8, 8), pl.ds(half * 128, 128)],
                     sem.at[part, half],
                 )
                 copy.start()
@@ -395,16 +424,21 @@
     )
 
 
+def exchange(near, far):
+    count = lax.axis_size("gx")
+    near = lax.ppermute(near, "gx", [(i, i ^ 1) for i in range(count)])
+    far = lax.ppermute(far, "gx", [(i, (i - 1 + 2 * (i % 2)) % count) for i in range(count)])
+    return near, far
+
+
 def block(east_class, south_class, cond_table, leakage, pad_mask, load):
-    gx, gy = lax.axis_size("gx"), lax.axis_size("gy")
-
-    def shift(values, axis, step):
-        count = gx if axis == "gx" else gy
-        return lax.ppermute(values, axis, [(i, (i + step) % count) for i in range(count)])
+    def shift(values, step):
+        count = lax.axis_size("gy")
+        return lax.ppermute(values, "gy", [(i, (i + step) % count) for i in range(count)])
 
     potential = pltpu.HBM((SIDE, SIDE, 256), F32)
     given = [pltpu.with_memory_space_constraint(a, pltpu.HBM) for a in (cond_table, east_class, south_class, leakage, pad_mask, load)]
-    right, left, to_down, to_up, tiny_down, tiny_up, te, ts, tx = call(
+    right, left, to_near, to_far, tiny_near, tiny_far, te, ts, tx = call(
         pack_kernel,
         [HBM] * 6,
         [pltpu.VMEM((MAIN_MSG, 128), F32)] * 4 + [pltpu.VMEM((TINY_MSG, 128), F32)] * 2 + [TURNED] * 3,
@@ -415,49 +449,47 @@
         1 << 22,
         4,
     )(*given)
-    tiny_from_up = shift(tiny_down, "gx", 1)
-    tiny_from_down = shift(tiny_up, "gx", -1)
-    from_up = shift(to_down, "gx", 1)
-    from_down = shift(to_up, "gx", -1)
+    tiny_one, tiny_other = exchange(tiny_near, tiny_far)
+    one, other = exchange(to_near, to_far)
     to_right, to_left, te2, ts2, tx2 = call(
         corner_kernel, [VMEM] * 7, [pltpu.VMEM((FULL_MSG, 128), F32)] * 2 + [TURNED] * 3, [VMEM] * 5, [], 1 << 20, 4
-    )(te, ts, tx, tiny_from_up, tiny_from_down, right, left)
-    from_left = shift(to_right, "gy", 1)
-    from_right = shift(to_left, "gy", -1)
+    )(te, ts, tx, tiny_one, tiny_other, right, left)
+    from_left = shift(to_right, 1)
+    from_right = shift(to_left, -1)
     s, x1, coef = call(
         first_kernel, [VMEM] * 3 + [HBM], [FIELD, FIELD, COEF], [VMEM] * 3, [FACTORS, DMA((SIDE // 8, 2))], 1 << 25, 4
     )(te, ts, tx, given[5])
-    *state, middle = call(
+    *state, out = call(
         main_kernel,
-        [VMEM] * 9,
-        [FIELD, FIELD, COEF, FIELD, FIELD, pltpu.VMEM((2, SIDE, SIDE, 128), F32)],
+        [VMEM] * 10,
+        [FIELD, FIELD, COEF, FIELD, FIELD, potential],
+        [VMEM] * 5 + [HBM],
+        [FACTORS, pltpu.VMEM((2, SIDE, SIDE, 128), F32), DMA((4, 2))],
+        1 << 25,
+        6,
+        {7 + i: i for i in range(3)},
+    )(te2, ts2, tx2, one, other, to_near, to_far, s, x1, coef)
+    strip = pltpu.VMEM((2, SIDE, 8, 128), F32)
+    *state, left_strip = call(
+        functools.partial(side_kernel, 0),
+        [VMEM] * 12,
+        [FIELD, FIELD, COEF, FIELD, FIELD, strip],
         [VMEM] * 6,
-        [FACTORS],
-        1 << 25,
-        4,
-        {6 + i: i for i in range(3)},
-    )(te2, ts2, tx2, from_up, from_down, to_up, s, x1, coef)
-    strip = pltpu.VMEM((2, SIDE, 8, 128), F32)
-    *state, out, right_strip = call(
-        functools.partial(side_kernel, 1),
-        [VMEM] * 10,
-        [FIELD, FIELD, COEF, FIELD, FIELD, potential, strip],
-        [VMEM] * 5 + [HBM, VMEM],
-        [TURNED] * 3 + [FACTORS, DMA((3, 2))],
+        [TURNED] * 3 + [FACTORS],
         1 << 23,
         4,
-        {5 + i: i for i in range(5)},
-    )(te2, ts2, tx2, from_right, middle, *state)
+        {7 + i: i for i in range(5)},
+    )(te2, ts2, tx2, from_left, left, one, other, *state)
     *state, out = call(
-        functools.partial(side_kernel, 0),
-        [VMEM] * 13 + [HBM],
+        functools.partial(side_kernel, 1),
+        [VMEM] * 10 + [HBM],
         [FIELD, FIELD, COEF, FIELD, FIELD, potential],
         [VMEM] * 5 + [HBM],
         [strip] + [TURNED] * 3 + [FACTORS, DMA((3, 2))],
         1 << 23,
         4,
-        {8 + i: i for i in range(6)},
-    )(te2, ts2, tx2, from_left, left, from_up, from_down, right_strip, *state, out)
+        {5 + i: i for i in range(6)},
+    )(te2, ts2, tx2, from_right, left_strip, *state, out)
     return out
 
 

time: 36.4 us -> 35.8 us (0.984)
  waiting for transfers between devices: 9.1 us -> 7.96 us
  starting transfers between devices: 10.4 us -> 10.9 us
    ppermute x6, waiting for transfers between devices: 9.1 us -> 7.96 us  [the longest x2 7.94 us: exchange(): lax.ppermute(far, 'gx', [(i, (i - 1 + 2 * (i % 2)) % count) for i in rang...]
    ppermute x6, starting transfers between devices: 10.4 us -> 10.9 us  [the longest x2 8.37 us: shift(): lax.ppermute(values, 'gy', [(i, (i + step) % count) for i in range(count)])]
  transfers between devices with their start and end apart: 6 -> 6, of which waited for: 3 -> 2; matrix products, arithmetic and copies ran while one was open for 0% -> 0% of each run, Pallas kernels for 33% -> 34%
where the time goes in v4:
time: 35.8 us; the launch traced here: 35.7 us
  Pallas kernels  16.8 us (47%)
  starting transfers between devices  10.9 us (30%)
  waiting for transfers between devices  7.96 us (22%)
    ppermute x2, starting transfers between devices, shift(): lax.ppermute(values, 'gy', [(i, (i + step) % count) for i in range(count)])  8.37 us
    ppermute x2, waiting for transfers between devices, exchange(): lax.ppermute(far, 'gx', [(i, (i - 1 + 2 * (i % 2)) % count) for i in rang...  7.94 us
    pallas_call x1, Pallas kernels, block(): call(main_kernel, [VMEM] * 10, [FIELD, FIELD, COEF, FIELD, FIELD, potenti...  5.88 us
    pallas_call x1, Pallas kernels, block(): call(first_kernel, [VMEM] * 3 + [HBM], [FIELD, FIELD, COEF], [VMEM] * 3,...  4.09 us
    pallas_call x1, Pallas kernels, block(): call(functools.partial(side_kernel, 1), [VMEM] * 10 + [HBM], [FIELD, FIEL...  2.77 us
    pallas_call x1, Pallas kernels, block(): call(functools.partial(side_kernel, 0), [VMEM] * 12, [FIELD, FIELD, COEF,...  2.03 us
    pallas_call x1, Pallas kernels, block(): call(pack_kernel, [HBM] * 6, [pltpu.VMEM((MAIN_MSG, 128), F32)] * 4 + [pl...  1.88 us
    ppermute x2, starting transfers between devices, exchange(): lax.ppermute(far, 'gx', [(i, (i - 1 + 2 * (i % 2)) % count) for i in rang...  1.77 us
  transfers between devices with their start and end apart: 6, of which 2 were waited for; matrix products, arithmetic and copies ran while one was open for 0% of the time, Pallas kernels for 34%

profile of v4, /device:TPU:7, one launch (start us, length us, event | category | flops | bytes accessed | tf_op | source)
XLA Modules:
  0.0 35.7 jit_solution(23026867333301519)
XLA Ops:
  0.0 1.9 %shard_map.64 = (f32[512,128]{1,0:T(8,128)S(1)}, f32[512,128]{1,0:T(8,128)S(1)}, f32[512,128]{1,0:T(8,128)S(1)}, f32[512,128]{1,0:T(8,128)S(1)}, f32[88,128]{1,0...) custom-call(f32[8]{0:T(128)} %refs_0_.1, ...), custom_call_target="tpu_custom_call" | custom-call | flops 4194304 | bytes 1048576 | tf_op jit(solution)/shard_map/pallas_call | solution.py:441
  1.9 0.8 %collective-permute-start = (f32[88,128]{1,0:T(8,128)S(1)}, f32[88,128]{1,0:T(8,128)S(1)}, u32[]{:S(2)}, u32[]{:S(2)}) collective-permute-start(f32[88,128]{1,0:T(8,128)S(1)} %get-tuple-element.38), channel_id=1, source_target_pairs={{0,16},{16,0},{32,48},{48,32},{64,80},{80,64},{96,112},{112,96},{1... | collective-permute-start | bytes 135176 | tf_op jit(solution)/shard_map/ppermute | solution.py:429
  2.7 1.2 %collective-permute-start.1 = (f32[88,128]{1,0:T(8,128)S(1)}, f32[88,128]{1,0:T(8,128)S(1)}, u32[]{:S(2)}, u32[]{:S(2)}) collective-permute-start(f32[88,128]{1,0:T(8,128)S(1)} %get-tuple-element.39), channel_id=1, source_target_pairs={{0,240},{16,32},{32,16},{48,64},{64,48},{80,96},{96,80},{112,128},... | collective-permute-start | bytes 135176 | tf_op jit(solution)/shard_map/ppermute | solution.py:430
  3.8 0.0 collective-permute-done.near
  3.9 4.4 %collective-permute-done.1.far = f32[88,128]{1,0:T(8,128)S(1)} collective-permute-done((f32[88,128]{1,0:T(8,128)S(1)}, f32[88,128]{1,0:T(8,128)S(1)}, u32[]{:S(2)}, u32[]{:S(2)}) %collective-permute-start.1) | collective-permute-done | bytes 45088 | tf_op jit(solution)/shard_map/ppermute | solution.py:430
  8.2 0.2 shard_map.65
  8.4 3.0 %collective-permute-start.3 = (f32[552,128]{1,0:T(8,128)S(1)}, f32[552,128]{1,0:T(8,128)S(1)}, u32[]{:S(2)}, u32[]{:S(2)}) collective-permute-start(f32[552,128]{1,0:T(8,128)S(1)} %get-tuple-element.46), channel_id=1, source_target_pairs={{0,1},{1,2},{2,3},{3,4},{4,5},{5,6},{6,7},{7,8},{8,9},{9,10},{10,1... | collective-permute-start | bytes 847880 | tf_op jit(solution)/shard_map/ppermute | solution.py:437
  11.4 5.4 %collective-permute-start.2 = (f32[552,128]{1,0:T(8,128)S(1)}, f32[552,128]{1,0:T(8,128)S(1)}, u32[]{:S(2)}, u32[]{:S(2)}) collective-permute-start(f32[552,128]{1,0:T(8,128)S(1)} %get-tuple-element.45), channel_id=1, source_target_pairs={{0,15},{1,0},{2,1},{3,2},{4,3},{5,4},{6,5},{7,6},{8,7},{9,8},{10,9... | collective-permute-start | bytes 847880 | tf_op jit(solution)/shard_map/ppermute | solution.py:437
  16.8 0.0 collective-permute-start.4
  16.8 0.6 %collective-permute-start.5 = (f32[512,128]{1,0:T(8,128)S(1)}, f32[512,128]{1,0:T(8,128)S(1)}, u32[]{:S(2)}, u32[]{:S(2)}) collective-permute-start(f32[512,128]{1,0:T(8,128)S(1)} %get-tuple-element.48.own_far), channel_id=1, source_target_pairs={{0,240},{16,32},{32,16},{48,64},{64,48},{80,96},{96,80},{112,128},... | collective-permute-start | bytes 786440 | tf_op jit(solution)/shard_map/ppermute | solution.py:430
  17.4 4.1 %shard_map.66 = (f32[2,72,80,128]{3,2,1,0:T(8,128)S(1)}, f32[2,72,80,128]{3,2,1,0:T(8,128)S(1)}, f32[3,72,80,128]{3,2,1,0:T(8,128)S(1)}) custom-call(f32[88,128]{1,0:T(8,128)S(1)} %get-tuple-element.35.te, f32[88,128]{1,0:T(8,128)S(1)} %get-tuple-element.36.ts, f32[88,128]{1,0:T(8,128)S(1)} %get-tuple-element.37.tx, f32[64,64,256]{2,1,0:T(8,128)} %load.1), custom_call_target="tpu_custom_call" | custom-call | flops 33554432 | bytes 1048576 | tf_op jit(solution)/shard_map/pallas_call | solution.py:459
  21.4 0.0 collective-permute-done.4.near.refs_5_
  21.5 3.6 %collective-permute-done.5.far.refs_6_ = f32[512,128]{1,0:T(8,128)S(1)} collective-permute-done((f32[512,128]{1,0:T(8,128)S(1)}, f32[512,128]{1,0:T(8,128)S(1)}, u32[]{:S(2)}, u32[]{:S(2)}) %collective-permute-start.5) | collective-permute-done | bytes 262176 | tf_op jit(solution)/shard_map/ppermute | solution.py:430
  25.0 5.9 %shard_map.67 = (f32[2,72,80,128]{3,2,1,0:T(8,128)S(1)}, f32[2,72,80,128]{3,2,1,0:T(8,128)S(1)}, f32[3,72,80,128]{3,2,1,0:T(8,128)S(1)}, f32[2,72,80,128]{3,2,1,...) custom-call(f32[88,128]{1,0:T(8,128)S(1)} %get-tuple-element.42.te.r, ...), custom_call_target="tpu_custom_call", output_to_operand_aliasing={{0}: (7, {}), {1}: (8, {}), {2}: (9, {})} | custom-call | flops 33554432 | bytes 1048576 | tf_op jit(solution)/shard_map/pallas_call | solution.py:462
  30.9 0.0 collective-permute-done.3.refs_3_
  30.9 2.0 %shard_map.68 = (f32[2,72,80,128]{3,2,1,0:T(8,128)S(1)}, f32[2,72,80,128]{3,2,1,0:T(8,128)S(1)}, f32[3,72,80,128]{3,2,1,0:T(8,128)S(1)}, f32[2,72,80,128]{3,2,1,...) custom-call(f32[88,128]{1,0:T(8,128)S(1)} %get-tuple-element.42.te.r, ...), custom_call_target="tpu_custom_call", output_to_operand_aliasing={{0}: (7, {}), {1}: (8, {}), {2}: (9, {}), {3}: (10, {}), {4... | custom-call | flops 8388608 | bytes 1048576 | tf_op jit(solution)/shard_map/pallas_call | solution.py:473
  33.0 0.0 collective-permute-done.2.refs_3_
  33.0 2.8 %shard_map.69 = (f32[2,72,80,128]{3,2,1,0:T(8,128)S(1)}, f32[2,72,80,128]{3,2,1,0:T(8,128)S(1)}, f32[3,72,80,128]{3,2,1,0:T(8,128)S(1)}, f32[2,72,80,128]{3,2,1,...) custom-call(f32[88,128]{1,0:T(8,128)S(1)} %get-tuple-element.42.te.r, ...), custom_call_target="tpu_custom_call", output_to_operand_aliasing={{0}: (5, {}), {1}: (6, {}), {2}: (7, {}), {3}: (8, {}), {4}... | custom-call | flops 8388608 | bytes 1048576 | tf_op jit(solution)/shard_map/pallas_call | solution.py:483
Async XLA Ops:
  1.9 2.0 %collective-permute-start = (f32[88,128]{1,0:T(8,128)S(1)}, f32[88,128]{1,0:T(8,128)S(1)}, u32[]{:S(2)}, u32[]{:S(2)}) collective-permute-start(f32[88,128]{1,0:T(8,128)S(1)} %get-tuple-element.38), channel_id=1, source_target_pairs={{0,16},{16,0},{32,48},{48,32},{64,80},{80,64},{96,112},{112,96},{1... | collective-permute-start | bytes 135176 | tf_op jit(solution)/shard_map/ppermute | solution.py:429
  2.7 5.6 %collective-permute-start.1 = (f32[88,128]{1,0:T(8,128)S(1)}, f32[88,128]{1,0:T(8,128)S(1)}, u32[]{:S(2)}, u32[]{:S(2)}) collective-permute-start(f32[88,128]{1,0:T(8,128)S(1)} %get-tuple-element.39), channel_id=1, source_target_pairs={{0,240},{16,32},{32,16},{48,64},{64,48},{80,96},{96,80},{112,128},... | collective-permute-start | bytes 135176 | tf_op jit(solution)/shard_map/ppermute | solution.py:430
  8.4 22.5 %collective-permute-start.3 = (f32[552,128]{1,0:T(8,128)S(1)}, f32[552,128]{1,0:T(8,128)S(1)}, u32[]{:S(2)}, u32[]{:S(2)}) collective-permute-start(f32[552,128]{1,0:T(8,128)S(1)} %get-tuple-element.46), channel_id=1, source_target_pairs={{0,1},{1,2},{2,3},{3,4},{4,5},{5,6},{6,7},{7,8},{8,9},{9,10},{10,1... | collective-permute-start | bytes 847880 | tf_op jit(solution)/shard_map/ppermute | solution.py:437
  11.4 21.6 %collective-permute-start.2 = (f32[552,128]{1,0:T(8,128)S(1)}, f32[552,128]{1,0:T(8,128)S(1)}, u32[]{:S(2)}, u32[]{:S(2)}) collective-permute-start(f32[552,128]{1,0:T(8,128)S(1)} %get-tuple-element.45), channel_id=1, source_target_pairs={{0,15},{1,0},{2,1},{3,2},{4,3},{5,4},{6,5},{7,6},{8,7},{9,8},{10,9... | collective-permute-start | bytes 847880 | tf_op jit(solution)/shard_map/ppermute | solution.py:437
  16.8 4.7 %collective-permute-start.4 = (f32[512,128]{1,0:T(8,128)S(1)}, f32[512,128]{1,0:T(8,128)S(1)}, u32[]{:S(2)}, u32[]{:S(2)}) collective-permute-start(f32[512,128]{1,0:T(8,128)S(1)} %get-tuple-element.47.own_near), channel_id=1, source_target_pairs={{0,16},{16,0},{32,48},{48,32},{64,80},{80,64},{96,112},{112,96},{1... | collective-permute-start | bytes 786440 | tf_op jit(solution)/shard_map/ppermute | solution.py:429
  16.8 8.2 %collective-permute-start.5 = (f32[512,128]{1,0:T(8,128)S(1)}, f32[512,128]{1,0:T(8,128)S(1)}, u32[]{:S(2)}, u32[]{:S(2)}) collective-permute-start(f32[512,128]{1,0:T(8,128)S(1)} %get-tuple-element.48.own_far), channel_id=1, source_target_pairs={{0,240},{16,32},{32,16},{48,64},{64,48},{80,96},{96,80},{112,128},... | collective-permute-start | bytes 786440 | tf_op jit(solution)/shard_map/ppermute | solution.py:430

commit v5 on v4

--- a/solution.py
+++ b/solution.py
@@ -227,27 +227,20 @@
     message[base + 13 : base + 16, :] = jnp.zeros((3, 128), F32)
 
 
-def first_kernel(te, ts, tx, load, s, x1, coef, factors, sem):
-    def part(group, half):
-        return pltpu.make_async_copy(
-            load.at[pl.ds(group * 8, 8), :, pl.ds(half * 128, 128)],
-            s.at[half, pl.ds(4 + group * 8, 8), pl.ds(8, SIDE), :],
-            sem.at[group, half],
-        )
-
-    for group in range(SIDE // 8):
-        for half in range(2):
-            part(group, half).start()
+def first_kernel(te, ts, tx, load, s, x1, coef, factors):
     own = range(8, SIDE + 8, 8)
     turn_factors(te, ts, tx, factors, own, own, own)
 
     def body(group, carry):
-        for half in range(2):
-            part(group, half).wait()
         for step in range(8):
             row = group * 8 + 4 + step
             for c in own:
-                to_source(s, row, c, set_factors(coef, row, all_at(c), factors, 8 + step))
+                signed = set_factors(coef, row, all_at(c), factors, 8 + step)
+                root = jnp.abs(signed)
+                supply = jnp.where(signed < 0.0, PAD_GAIN, 0.0)
+                for half in range(2):
+                    drawn = load[row - 4, c - 8 : c, half * 128 : half * 128 + 128]
+                    s[half, row, c : c + 8, :] = (supply - drawn) * root
         for c in own:
             neighbours(s, coef, group * 8 + 3, 8, c, adding(x1))
             for which in range(3):
@@ -284,7 +277,7 @@
 
 
 def main_kernel(te, ts, tx, near, far, own_near, own_far, *rest):
-    s, x1, coef, u, t, out, factors, done, sem = rest[3:]
+    s, x1, coef, u, t, done, factors = rest[3:]
     even = even_row()
     own = range(8, SIDE + 8, 8)
     turn_factors(te, ts, tx, factors, own, own, own)
@@ -309,36 +302,23 @@
     def finish(half, row, c, total, here):
         done[half, row - 4, c - 8 : c, :] = result(s, u, coef, half, row, c, total)
 
-    outs = []
-    for part in range(4):
-        rows = pl.ds(part * 16, 16)
-        sweep(t, coef, 4 + part * 16, 20 + part * 16, range(16, SIDE, 8), 16, finish)
-        for half in range(2):
-            copy = pltpu.make_async_copy(
-                done.at[half, rows, pl.ds(8, SIDE - 16), :],
-                out.at[rows, pl.ds(8, SIDE - 16), pl.ds(half * 128, 128)],
-                sem.at[part, half],
-            )
-            copy.start()
-            outs.append(copy)
-    for copy in outs:
-        copy.wait()
+    sweep(t, coef, 4, SIDE + 4, range(16, SIDE, 8), 16, finish)
 
 
 def side_kernel(side, *refs):
     te2, ts2, tx2, message = refs[:4]
-    if side:
-        s, x1, coef, u, t, out, done, te, ts, tx, factors, sem = refs[-12:]
-    else:
-        s, x1, coef, u, t, done, te, ts, tx, factors = refs[-10:]
+    s, x1, coef, u, t, out, done, te, ts, tx, factors, sem = refs[-12:]
+    ready = refs[4 if side else 7]
+    first, width = (0, 8) if side else (8, SIDE - 16)
     outs = []
-    if side:
-        for half in range(2):
-            copy = pltpu.make_async_copy(
-                refs[4].at[half], out.at[:, pl.ds(0, 8), pl.ds(half * 128, 128)], sem.at[2, half]
-            )
-            copy.start()
-            outs.append(copy)
+    for half in range(2):
+        copy = pltpu.make_async_copy(
+            ready.at[half] if side else ready.at[half, :, pl.ds(8, width), :],
+            out.at[:, pl.ds(first, width), pl.ds(half * 128, 128)],
+            sem.at[4, half],
+        )
+        copy.start()
+        outs.append(copy)
     for source, target in ((te2, te), (ts2, ts), (tx2, tx)):
         target[...] = source[...]
     at = MAIN_MSG + 24
@@ -370,25 +350,31 @@
         start = SIDE + 8 if side else 8 - count
         s[half, row, start : start + count, :] = message[MAIN_MSG + offset : MAIN_MSG + offset + count, :]
 
-    def body(group, carry):
+    window = SIDE + 4 if side else 4
+
+    def factor_rows(base):
         for step in range(8):
-            row = group * 8 + step
-            to_source(s, row, c, set_factors(coef, row, places, factors, 4 + step))
+            to_source(s, base + step, c, set_factors(coef, base + step, places, factors, 4 + step))
         for which, k in places:
             factors[which, k : k + 8, :] = pltpu.roll(factors[which, k : k + 8, :], 120, 1)
+
+    def body(group, carry):
+        factor_rows(group * 8)
+        neighbours(s, coef, group * 8 - 1, 8, window, adding(x1))
         return carry
 
-    lax.fori_loop(0, ROWS // 8, body, 0)
-    sweep(s, coef, 1, SIDE + 7, (SIDE + 4 if side else 4,), 14, adding(x1))
+    factor_rows(0)
+    neighbours(s, coef, 1, 6, window, adding(x1))
+    lax.fori_loop(1, ROWS // 8, body, 0)
     sweep(x1, coef, 2, SIDE + 6, (SIDE + 3 if side else 5,), 17, placing(u))
     sweep(u, coef, 3, SIDE + 5, (SIDE + 2 if side else 6,), 22, placing(t))
 
     def finish(half, row, c, total, here):
         done[half, row - 4, :, :] = result(s, u, coef, half, row, c, total)
 
-    for part in range(2):
-        rows = pl.ds(part * (SIDE // 2), SIDE // 2)
-        sweep(t, coef, 4 + part * (SIDE // 2), 4 + (part + 1) * (SIDE // 2), (SIDE if side else 8,), 16, finish)
+    for part in range(4):
+        rows = pl.ds(part * 16, 16)
+        sweep(t, coef, 4 + part * 16, 20 + part * 16, (SIDE if side else 8,), 16, finish)
         for half in range(2):
             if side:
                 copy = pltpu.make_async_copy(
@@ -426,8 +412,8 @@
 
 def exchange(near, far):
     count = lax.axis_size("gx")
+    far = lax.ppermute(far, "gx", [(i, (i - 1 + 2 * (i % 2)) % count) for i in range(count)])
     near = lax.ppermute(near, "gx", [(i, i ^ 1) for i in range(count)])
-    far = lax.ppermute(far, "gx", [(i, (i - 1 + 2 * (i % 2)) % count) for i in range(count)])
     return near, far
 
 
@@ -449,6 +435,7 @@
         1 << 22,
         4,
     )(*given)
+    late = lax.optimization_barrier((load, te))[0]
     tiny_one, tiny_other = exchange(tiny_near, tiny_far)
     one, other = exchange(to_near, to_far)
     to_right, to_left, te2, ts2, tx2 = call(
@@ -457,35 +444,35 @@
     from_left = shift(to_right, 1)
     from_right = shift(to_left, -1)
     s, x1, coef = call(
-        first_kernel, [VMEM] * 3 + [HBM], [FIELD, FIELD, COEF], [VMEM] * 3, [FACTORS, DMA((SIDE // 8, 2))], 1 << 25, 4
-    )(te, ts, tx, given[5])
-    *state, out = call(
+        first_kernel, [VMEM] * 4, [FIELD, FIELD, COEF], [VMEM] * 3, [FACTORS], 1 << 25, 4
+    )(te, ts, tx, pltpu.with_memory_space_constraint(late, pltpu.VMEM))
+    *state, middle = call(
         main_kernel,
         [VMEM] * 10,
-        [FIELD, FIELD, COEF, FIELD, FIELD, potential],
-        [VMEM] * 5 + [HBM],
-        [FACTORS, pltpu.VMEM((2, SIDE, SIDE, 128), F32), DMA((4, 2))],
+        [FIELD, FIELD, COEF, FIELD, FIELD, pltpu.VMEM((2, SIDE, SIDE, 128), F32)],
+        [VMEM] * 6,
+        [FACTORS],
         1 << 25,
-        6,
+        4,
         {7 + i: i for i in range(3)},
     )(te2, ts2, tx2, one, other, to_near, to_far, s, x1, coef)
     strip = pltpu.VMEM((2, SIDE, 8, 128), F32)
-    *state, left_strip = call(
+    *state, out, left_strip = call(
         functools.partial(side_kernel, 0),
-        [VMEM] * 12,
-        [FIELD, FIELD, COEF, FIELD, FIELD, strip],
-        [VMEM] * 6,
-        [TURNED] * 3 + [FACTORS],
+        [VMEM] * 13,
+        [FIELD, FIELD, COEF, FIELD, FIELD, potential, strip],
+        [VMEM] * 5 + [HBM, VMEM],
+        [TURNED] * 3 + [FACTORS, DMA((5, 2))],
         1 << 23,
         4,
-        {7 + i: i for i in range(5)},
-    )(te2, ts2, tx2, from_left, left, one, other, *state)
+        {8 + i: i for i in range(5)},
+    )(te2, ts2, tx2, from_left, left, one, other, middle, *state)
     *state, out = call(
         functools.partial(side_kernel, 1),
         [VMEM] * 10 + [HBM],
         [FIELD, FIELD, COEF, FIELD, FIELD, potential],
         [VMEM] * 5 + [HBM],
-        [strip] + [TURNED] * 3 + [FACTORS, DMA((3, 2))],
+        [strip] + [TURNED] * 3 + [FACTORS, DMA((5, 2))],
         1 << 23,
         4,
         {5 + i: i for i in range(6)},

time: 35.8 us -> 35.9 us (level)
  waiting for transfers between devices: 7.96 us -> 8.77 us
  Pallas kernels: 16.8 us -> 16.1 us
    pallas_call x3, Pallas kernels: 12 us -> 11.1 us  [the longest x1 5.64 us: block(): call(main_kernel, [VMEM] * 10, [FIELD, FIELD, COEF, FIELD, FIELD, pltpu.V...]
    ppermute x2, waiting for transfers between devices: 7.94 us -> 8.76 us  [exchange(): lax.ppermute(far, 'gx', [(i, (i - 1 + 2 * (i % 2)) % count) for i in rang...]
  transfers between devices with their start and end apart: 6 -> 6, of which waited for: 2 -> 2; matrix products, arithmetic and copies ran while one was open for 0% -> 0% of each run, Pallas kernels for 34% -> 31%
where the time goes in v5:
time: 35.9 us; the launch traced here: 35.8 us
  Pallas kernels  16.1 us (45%)
  starting transfers between devices  10.9 us (30%)
  waiting for transfers between devices  8.77 us (24%)
    ppermute x2, waiting for transfers between devices, exchange(): lax.ppermute(far, 'gx', [(i, (i - 1 + 2 * (i % 2)) % count) for i in rang...  8.76 us
    ppermute x2, starting transfers between devices, shift(): lax.ppermute(values, 'gy', [(i, (i + step) % count) for i in range(count)])  8.37 us
    pallas_call x1, Pallas kernels, block(): call(main_kernel, [VMEM] * 10, [FIELD, FIELD, COEF, FIELD, FIELD, pltpu.V...  5.64 us
    pallas_call x1, Pallas kernels, block(): call(first_kernel, [VMEM] * 4, [FIELD, FIELD, COEF], [VMEM] * 3, [FACTORS...  3.27 us
    pallas_call x1, Pallas kernels, block(): call(functools.partial(side_kernel, 1), [VMEM] * 10 + [HBM], [FIELD, FIEL...  2.77 us
    pallas_call x1, Pallas kernels, block(): call(functools.partial(side_kernel, 0), [VMEM] * 13, [FIELD, FIELD, COEF,...  2.22 us
    pallas_call x1, Pallas kernels, block(): call(pack_kernel, [HBM] * 6, [pltpu.VMEM((MAIN_MSG, 128), F32)] * 4 + [pl...  2.03 us
    ppermute x2, starting transfers between devices, exchange(): lax.ppermute(far, 'gx', [(i, (i - 1 + 2 * (i % 2)) % count) for i in rang...  1.77 us
  transfers between devices with their start and end apart: 6, of which 2 were waited for; matrix products, arithmetic and copies ran while one was open for 0% of the time, Pallas kernels for 31%

profile of v5, /device:TPU:7, one launch (start us, length us, event | category | flops | bytes accessed | tf_op | source)
XLA Modules:
  0.0 35.8 jit_solution(4184504104203796240)
XLA Ops:
  0.0 0.0 copy-start
  0.0 2.0 %shard_map.64 = (f32[512,128]{1,0:T(8,128)S(1)}, f32[512,128]{1,0:T(8,128)S(1)}, f32[512,128]{1,0:T(8,128)S(1)}, f32[512,128]{1,0:T(8,128)S(1)}, f32[88,128]{1,0...) custom-call(f32[8]{0:T(128)} %refs_0_.1, ...), custom_call_target="tpu_custom_call" | custom-call | flops 4194304 | bytes 1048576 | tf_op jit(solution)/shard_map/pallas_call | solution.py:427
  2.0 0.8 %collective-permute-start = (f32[88,128]{1,0:T(8,128)S(1)}, f32[88,128]{1,0:T(8,128)S(1)}, u32[]{:S(2)}, u32[]{:S(2)}) collective-permute-start(f32[88,128]{1,0:T(8,128)S(1)} %get-tuple-element.40), channel_id=1, source_target_pairs={{0,16},{16,0},{32,48},{48,32},{64,80},{80,64},{96,112},{112,96},{1... | collective-permute-start | bytes 135176 | tf_op jit(solution)/shard_map/ppermute | solution.py:416
  2.8 1.2 %collective-permute-start.1 = (f32[88,128]{1,0:T(8,128)S(1)}, f32[88,128]{1,0:T(8,128)S(1)}, u32[]{:S(2)}, u32[]{:S(2)}) collective-permute-start(f32[88,128]{1,0:T(8,128)S(1)} %get-tuple-element.41), channel_id=1, source_target_pairs={{0,240},{16,32},{32,16},{48,64},{64,48},{80,96},{96,80},{112,128},... | collective-permute-start | bytes 135176 | tf_op jit(solution)/shard_map/ppermute | solution.py:415
  4.0 0.0 collective-permute-done.near
  4.0 4.4 %collective-permute-done.1.far = f32[88,128]{1,0:T(8,128)S(1)} collective-permute-done((f32[88,128]{1,0:T(8,128)S(1)}, f32[88,128]{1,0:T(8,128)S(1)}, u32[]{:S(2)}, u32[]{:S(2)}) %collective-permute-start.1) | collective-permute-done | bytes 45088 | tf_op jit(solution)/shard_map/ppermute | solution.py:415
  8.4 0.2 shard_map.65
  8.5 3.0 %collective-permute-start.3 = (f32[552,128]{1,0:T(8,128)S(1)}, f32[552,128]{1,0:T(8,128)S(1)}, u32[]{:S(2)}, u32[]{:S(2)}) collective-permute-start(f32[552,128]{1,0:T(8,128)S(1)} %get-tuple-element.48), channel_id=1, source_target_pairs={{0,1},{1,2},{2,3},{3,4},{4,5},{5,6},{6,7},{7,8},{8,9},{9,10},{10,1... | collective-permute-start | bytes 847880 | tf_op jit(solution)/shard_map/ppermute | solution.py:423
  11.5 5.4 %collective-permute-start.2 = (f32[552,128]{1,0:T(8,128)S(1)}, f32[552,128]{1,0:T(8,128)S(1)}, u32[]{:S(2)}, u32[]{:S(2)}) collective-permute-start(f32[552,128]{1,0:T(8,128)S(1)} %get-tuple-element.47), channel_id=1, source_target_pairs={{0,15},{1,0},{2,1},{3,2},{4,3},{5,4},{6,5},{7,6},{8,7},{9,8},{10,9... | collective-permute-start | bytes 847880 | tf_op jit(solution)/shard_map/ppermute | solution.py:423
  16.9 0.0 collective-permute-start.4
  16.9 0.6 %collective-permute-start.5 = (f32[512,128]{1,0:T(8,128)S(1)}, f32[512,128]{1,0:T(8,128)S(1)}, u32[]{:S(2)}, u32[]{:S(2)}) collective-permute-start(f32[512,128]{1,0:T(8,128)S(1)} %get-tuple-element.50.own_far), channel_id=1, source_target_pairs={{0,240},{16,32},{32,16},{48,64},{64,48},{80,96},{96,80},{112,128},... | collective-permute-start | bytes 786440 | tf_op jit(solution)/shard_map/ppermute | solution.py:415
  17.5 0.0 copy-done
  17.5 3.3 %shard_map.66 = (f32[2,72,80,128]{3,2,1,0:T(8,128)S(1)}, f32[2,72,80,128]{3,2,1,0:T(8,128)S(1)}, f32[3,72,80,128]{3,2,1,0:T(8,128)S(1)}) custom-call(f32[88,128]{1,0:T(8,128)S(1)} %get-tuple-element.37.te, f32[88,128]{1,0:T(8,128)S(1)} %get-tuple-element.38.ts, f32[88,128]{1,0:T(8,128)S(1)} %get-tuple-element.39.tx, f32[64,64,256]{2,1,0:T(8,128)S(1)} %copy-done), custom_call_target="tpu_custom_call" | custom-call | flops 33554432 | bytes 1048576 | tf_op jit(solution)/shard_map/pallas_call | solution.py:446
  20.8 0.0 collective-permute-done.4.near.refs_5_
  20.8 4.4 %collective-permute-done.5.far.refs_6_ = f32[512,128]{1,0:T(8,128)S(1)} collective-permute-done((f32[512,128]{1,0:T(8,128)S(1)}, f32[512,128]{1,0:T(8,128)S(1)}, u32[]{:S(2)}, u32[]{:S(2)}) %collective-permute-start.5) | collective-permute-done | bytes 262176 | tf_op jit(solution)/shard_map/ppermute | solution.py:415
  25.2 5.6 %shard_map.67 = (f32[2,72,80,128]{3,2,1,0:T(8,128)S(1)}, f32[2,72,80,128]{3,2,1,0:T(8,128)S(1)}, f32[3,72,80,128]{3,2,1,0:T(8,128)S(1)}, f32[2,72,80,128]{3,2,1,...) custom-call(f32[88,128]{1,0:T(8,128)S(1)} %get-tuple-element.44.te.r, ...), custom_call_target="tpu_custom_call", output_to_operand_aliasing={{0}: (7, {}), {1}: (8, {}), {2}: (9, {})} | custom-call | flops 33554432 | bytes 1048576 | tf_op jit(solution)/shard_map/pallas_call | solution.py:449
  30.8 0.0 collective-permute-done.3.refs_3_
  30.8 2.2 %shard_map.68 = (f32[2,72,80,128]{3,2,1,0:T(8,128)S(1)}, f32[2,72,80,128]{3,2,1,0:T(8,128)S(1)}, f32[3,72,80,128]{3,2,1,0:T(8,128)S(1)}, f32[2,72,80,128]{3,2,1,...) custom-call(f32[88,128]{1,0:T(8,128)S(1)} %get-tuple-element.44.te.r, ...), custom_call_target="tpu_custom_call", output_to_operand_aliasing={{0}: (8, {}), {1}: (9, {}), {2}: (10, {}), {3}: (11, {}), {... | custom-call | flops 8388608 | bytes 1048576 | tf_op jit(solution)/shard_map/pallas_call | solution.py:460
  33.1 0.0 collective-permute-done.2.refs_3_
  33.1 2.8 %shard_map.69 = (f32[2,72,80,128]{3,2,1,0:T(8,128)S(1)}, f32[2,72,80,128]{3,2,1,0:T(8,128)S(1)}, f32[3,72,80,128]{3,2,1,0:T(8,128)S(1)}, f32[2,72,80,128]{3,2,1,...) custom-call(f32[88,128]{1,0:T(8,128)S(1)} %get-tuple-element.44.te.r, ...), custom_call_target="tpu_custom_call", output_to_operand_aliasing={{0}: (5, {}), {1}: (6, {}), {2}: (7, {}), {3}: (8, {}), {4}... | custom-call | flops 8388608 | bytes 1048576 | tf_op jit(solution)/shard_map/pallas_call | solution.py:470
Async XLA Ops:
  0.0 17.5 %copy-start = (f32[64,64,256]{2,1,0:T(8,128)S(1)}, f32[64,64,256]{2,1,0:T(8,128)}, u32[]{:S(2)}) copy-start(f32[64,64,256]{2,1,0:T(8,128)} %load) | copy-start | bytes 12582916
  2.0 2.0 %collective-permute-start = (f32[88,128]{1,0:T(8,128)S(1)}, f32[88,128]{1,0:T(8,128)S(1)}, u32[]{:S(2)}, u32[]{:S(2)}) collective-permute-start(f32[88,128]{1,0:T(8,128)S(1)} %get-tuple-element.40), channel_id=1, source_target_pairs={{0,16},{16,0},{32,48},{48,32},{64,80},{80,64},{96,112},{112,96},{1... | collective-permute-start | bytes 135176 | tf_op jit(solution)/shard_map/ppermute | solution.py:416
  2.8 5.6 %collective-permute-start.1 = (f32[88,128]{1,0:T(8,128)S(1)}, f32[88,128]{1,0:T(8,128)S(1)}, u32[]{:S(2)}, u32[]{:S(2)}) collective-permute-start(f32[88,128]{1,0:T(8,128)S(1)} %get-tuple-element.41), channel_id=1, source_target_pairs={{0,240},{16,32},{32,16},{48,64},{64,48},{80,96},{96,80},{112,128},... | collective-permute-start | bytes 135176 | tf_op jit(solution)/shard_map/ppermute | solution.py:415
  8.5 22.3 %collective-permute-start.3 = (f32[552,128]{1,0:T(8,128)S(1)}, f32[552,128]{1,0:T(8,128)S(1)}, u32[]{:S(2)}, u32[]{:S(2)}) collective-permute-start(f32[552,128]{1,0:T(8,128)S(1)} %get-tuple-element.48), channel_id=1, source_target_pairs={{0,1},{1,2},{2,3},{3,4},{4,5},{5,6},{6,7},{7,8},{8,9},{9,10},{10,1... | collective-permute-start | bytes 847880 | tf_op jit(solution)/shard_map/ppermute | solution.py:423
  11.5 21.5 %collective-permute-start.2 = (f32[552,128]{1,0:T(8,128)S(1)}, f32[552,128]{1,0:T(8,128)S(1)}, u32[]{:S(2)}, u32[]{:S(2)}) collective-permute-start(f32[552,128]{1,0:T(8,128)S(1)} %get-tuple-element.47), channel_id=1, source_target_pairs={{0,15},{1,0},{2,1},{3,2},{4,3},{5,4},{6,5},{7,6},{8,7},{9,8},{10,9... | collective-permute-start | bytes 847880 | tf_op jit(solution)/shard_map/ppermute | solution.py:423
  16.9 3.9 %collective-permute-start.4 = (f32[512,128]{1,0:T(8,128)S(1)}, f32[512,128]{1,0:T(8,128)S(1)}, u32[]{:S(2)}, u32[]{:S(2)}) collective-permute-start(f32[512,128]{1,0:T(8,128)S(1)} %get-tuple-element.49.own_near), channel_id=1, source_target_pairs={{0,16},{16,0},{32,48},{48,32},{64,80},{80,64},{96,112},{112,96},{1... | collective-permute-start | bytes 786440 | tf_op jit(solution)/shard_map/ppermute | solution.py:416
  16.9 8.2 %collective-permute-start.5 = (f32[512,128]{1,0:T(8,128)S(1)}, f32[512,128]{1,0:T(8,128)S(1)}, u32[]{:S(2)}, u32[]{:S(2)}) collective-permute-start(f32[512,128]{1,0:T(8,128)S(1)} %get-tuple-element.50.own_far), channel_id=1, source_target_pairs={{0,240},{16,32},{32,16},{48,64},{64,48},{80,96},{96,80},{112,128},... | collective-permute-start | bytes 786440 | tf_op jit(solution)/shard_map/ppermute | solution.py:415

commit v6 on v5

--- a/solution.py
+++ b/solution.py
@@ -16,7 +16,7 @@
 ROWS = SIDE + 8
 COLS = SIDE + 16
 MAIN_MSG = 8 * SIDE
-TINY_MSG = SIDE + 24
+TINY_MSG = 16 + 24
 FULL_MSG = MAIN_MSG + 24 + 16
 TURNED_ROWS = SIDE + 24
 F32 = jnp.float32
@@ -154,23 +154,13 @@
     for copy in nodes:
         copy.start()
     for side in range(2):
-        for half in range(2):
-            copy = pltpu.make_async_copy(
-                load.at[:, pl.ds(side * (SIDE - 8), 8), pl.ds(half * 128, 128)], edge.at[side, half], sem_edge.at[side, half]
-            )
-            copy.start()
-            edges.append(copy)
+        copy = pltpu.make_async_copy(load.at[:, pl.ds(side * (SIDE - 8), 8), :], edge.at[side], sem_edge.at[side])
+        copy.start()
+        edges.append(copy)
     for place, (start, message) in enumerate(((near, to_near), (far, to_far))):
-        for half in range(2):
-            for row in range(4):
-                copy = pltpu.make_async_copy(
-                    load.at[start + row, :, pl.ds(half * 128, 128)],
-                    message.at[pl.ds((half * 4 + row) * SIDE, SIDE), :],
-                    sem_rows.at[place, half, row],
-                )
-                copy.start()
-                tops.append(copy)
-
+        copy = pltpu.make_async_copy(load.at[pl.ds(start, 4)], message.at[pl.ds(0, 4)], sem_rows.at[place])
+        copy.start()
+        tops.append(copy)
     for copy in nodes:
         copy.wait()
 
@@ -201,21 +191,28 @@
         return jnp.where(lane < 8, first, jnp.where(lane < 16, second, third))
 
     lower, upper = banded((64, 72, 80)), banded((120, 0, 8))
-    tiny_near[0:SIDE, :] = jnp.where(even, lower, upper)
-    tiny_far[0:SIDE, :] = jnp.where(even, upper, lower)
+    for tiny, message, banded_rows in (
+        (tiny_near, to_near, jnp.where(even, lower, upper)),
+        (tiny_far, to_far, jnp.where(even, upper, lower)),
+    ):
+        message[4, :, 0:128] = banded_rows
+        message[4, :, 128:256] = jnp.zeros((SIDE, 128), F32)
+        tiny[0:8, :] = banded_rows[0:8, :]
+        tiny[8:16, :] = banded_rows[SIDE - 8 :, :]
     for copy in edges:
         copy.wait()
     for offset, half, side, distance in corner_cells():
         count = 4 - distance
-        at = SIDE + offset
+        at = 16 + offset
+        lanes = slice(half * 128, half * 128 + 128)
         columns = slice(8 - count, 8) if side else slice(0, count)
-        tiny_near[at : at + count, :] = edge[side, half, jnp.where(even, SIDE - distance, distance - 1), columns, :]
-        tiny_far[at : at + count, :] = edge[side, half, jnp.where(even, distance - 1, SIDE - distance), columns, :]
+        tiny_near[at : at + count, :] = edge[side, jnp.where(even, SIDE - distance, distance - 1), columns, lanes]
+        tiny_far[at : at + count, :] = edge[side, jnp.where(even, distance - 1, SIDE - distance), columns, lanes]
     for side, message in enumerate((to_left, to_right)):
         for half in range(2):
             for row in range(SIDE):
                 base = (half * SIDE + row) * 4
-                message[base : base + 4, :] = edge[side, half, row, side * 4 : side * 4 + 4, :]
+                message[base : base + 4, :] = edge[side, row, side * 4 : side * 4 + 4, half * 128 : half * 128 + 128]
     for copy in tops:
         copy.wait()
 
@@ -250,24 +247,29 @@
     lax.fori_loop(0, SIDE // 8, body, 0)
 
 
+def widen(te, ts, tx, first, count, upper, lower):
+    lane = lanes_of((count, 128))
+    for target, down, up in ((te, 0, 72), (ts, 120, 64), (tx, 112, 56)):
+        head = pltpu.roll(upper, down, 1) if down else upper
+        own = target[first : first + count, :]
+        target[first : first + count, :] = jnp.where(
+            lane < 8, head, jnp.where(lane < SIDE + 8, own, pltpu.roll(lower, up, 1))
+        )
+
+
 def corner_kernel(te, ts, tx, near, far, right, left, to_right, to_left, te2, ts2, tx2):
-    lane = lanes_of((SIDE, 128))
     even = even_row()
-    upper = jnp.where(even, far[0:SIDE, :], near[0:SIDE, :])
-    lower = jnp.where(even, near[0:SIDE, :], far[0:SIDE, :])
-    for source, target, down, up in ((te, te2, 0, 72), (ts, ts2, 120, 64), (tx, tx2, 112, 56)):
-        head = pltpu.roll(upper, down, 1) if down else upper
-        tail = pltpu.roll(lower, up, 1)
-        own = source[8 : SIDE + 8, :]
-        target[0:8, :] = jnp.zeros((8, 128), F32)
-        target[8 : SIDE + 8, :] = jnp.where(lane < 8, head, jnp.where(lane < SIDE + 8, own, tail))
-        target[SIDE + 8 :, :] = jnp.zeros((16, 128), F32)
+    for source, target in ((te, te2), (ts, ts2), (tx, tx2)):
+        target[...] = source[...]
+    for at, first in ((0, 8), (8, SIDE)):
+        one, other = near[at : at + 8, :], far[at : at + 8, :]
+        widen(te2, ts2, tx2, first, 8, jnp.where(even, other, one), jnp.where(even, one, other))
     to_right[0:MAIN_MSG, :] = right[...]
     to_left[0:MAIN_MSG, :] = left[...]
     for offset, half, below, distance in corner_cells():
         count = 4 - distance
         for side, message in enumerate((to_left, to_right)):
-            at = SIDE + (half * 2 + side) * 6 + (0, 3, 5)[distance - 1]
+            at = 16 + (half * 2 + side) * 6 + (0, 3, 5)[distance - 1]
             first, second = (near, far) if below else (far, near)
             message[MAIN_MSG + offset : MAIN_MSG + offset + count, :] = jnp.where(
                 even, first[at : at + count, :], second[at : at + count, :]
@@ -276,19 +278,22 @@
     put_conductances(to_left, MAIN_MSG + 24, te2, ts2, tx2, 8, 8)
 
 
-def main_kernel(te, ts, tx, near, far, own_near, own_far, *rest):
-    s, x1, coef, u, t, done, factors = rest[3:]
+def main_kernel(own_te, own_ts, own_tx, near, far, own_near, own_far, *rest):
+    s, x1, coef, u, t, done, te, ts, tx, factors = rest[3:]
     even = even_row()
+    for source, target in ((own_te, te), (own_ts, ts), (own_tx, tx)):
+        target[...] = source[...]
+    one, other = near[4, :, 0:128], far[4, :, 0:128]
+    widen(te, ts, tx, 8, SIDE, jnp.where(even, other, one), jnp.where(even, one, other))
     own = range(8, SIDE + 8, 8)
     turn_factors(te, ts, tx, factors, own, own, own)
     for half in range(2):
         for row in range(4):
-            at = (half * 4 + row) * SIDE
-            one, other = near[at : at + SIDE, :], far[at : at + SIDE, :]
+            lanes = slice(half * 128, half * 128 + 128)
+            one, other = near[row, :, lanes], far[row, :, lanes]
             s[half, row, 8 : SIDE + 8, :] = jnp.where(even, other, one)
             s[half, SIDE + 4 + row, 8 : SIDE + 8, :] = jnp.where(even, one, other)
-        at = half * 4 * SIDE
-        s[half, 4, 8 : SIDE + 8, :] = jnp.where(even, own_far[at : at + SIDE, :], own_near[at : at + SIDE, :])
+        s[half, 4, 8 : SIDE + 8, :] = jnp.where(even, own_far[0, :, lanes], own_near[0, :, lanes])
     for row in (0, 1, 2, 3, 4, SIDE + 3, SIDE + 4, SIDE + 5, SIDE + 6, SIDE + 7):
         for c in own:
             signed = set_factors(coef, row, all_at(c), factors, row + 4)
@@ -308,17 +313,23 @@
 def side_kernel(side, *refs):
     te2, ts2, tx2, message = refs[:4]
     s, x1, coef, u, t, out, done, te, ts, tx, factors, sem = refs[-12:]
-    ready = refs[4 if side else 7]
-    first, width = (0, 8) if side else (8, SIDE - 16)
-    outs = []
-    for half in range(2):
-        copy = pltpu.make_async_copy(
-            ready.at[half] if side else ready.at[half, :, pl.ds(8, width), :],
-            out.at[:, pl.ds(first, width), pl.ds(half * 128, 128)],
-            sem.at[4, half],
+    middle = refs[4 if side else 7]
+    outs = [
+        pltpu.make_async_copy(
+            middle.at[side, :, pl.ds(8, SIDE - 16), :],
+            out.at[:, pl.ds(8, SIDE - 16), pl.ds(side * 128, 128)],
+            sem.at[4, 0],
         )
+    ]
+    if side:
+        for half in range(2):
+            outs.append(
+                pltpu.make_async_copy(
+                    refs[5].at[half], out.at[:, pl.ds(0, 8), pl.ds(half * 128, 128)], sem.at[4, 1 + half]
+                )
+            )
+    for copy in outs:
         copy.start()
-        outs.append(copy)
     for source, target in ((te2, te), (ts2, ts), (tx2, tx)):
         target[...] = source[...]
     at = MAIN_MSG + 24
@@ -340,8 +351,8 @@
         even = even_row()
         for half in range(2):
             for row in range(4):
-                at = (half * 4 + row) * SIDE
-                one, other = refs[5][at : at + 1, :], refs[6][at : at + 1, :]
+                lanes = slice(half * 128, half * 128 + 128)
+                one, other = refs[5][row, 0:1, lanes], refs[6][row, 0:1, lanes]
                 s[half, row, 8:9, :] = jnp.where(even, other, one)
                 s[half, SIDE + 4 + row, 8:9, :] = jnp.where(even, one, other)
     for offset, half, below, distance in corner_cells():
@@ -352,22 +363,15 @@
 
     window = SIDE + 4 if side else 4
 
-    def factor_rows(base):
-        for step in range(8):
-            to_source(s, base + step, c, set_factors(coef, base + step, places, factors, 4 + step))
-        for which, k in places:
-            factors[which, k : k + 8, :] = pltpu.roll(factors[which, k : k + 8, :], 120, 1)
-
-    def body(group, carry):
-        factor_rows(group * 8)
-        neighbours(s, coef, group * 8 - 1, 8, window, adding(x1))
-        return carry
-
-    factor_rows(0)
-    neighbours(s, coef, 1, 6, window, adding(x1))
-    lax.fori_loop(1, ROWS // 8, body, 0)
-    sweep(x1, coef, 2, SIDE + 6, (SIDE + 3 if side else 5,), 17, placing(u))
-    sweep(u, coef, 3, SIDE + 5, (SIDE + 2 if side else 6,), 22, placing(t))
+    for group in range(ROWS // 8):
+        for row in range(group * 8, group * 8 + 8):
+            to_source(s, row, c, set_factors(coef, row, places, factors, row + 4))
+        if group == 0:
+            neighbours(s, coef, 1, 6, window, adding(x1))
+        else:
+            neighbours(s, coef, group * 8 - 1, 8, window, adding(x1))
+    sweep(x1, coef, 2, SIDE + 6, (SIDE + 3 if side else 5,), 34, placing(u))
+    sweep(u, coef, 3, SIDE + 5, (SIDE + 2 if side else 6,), 33, placing(t))
 
     def finish(half, row, c, total, here):
         done[half, row - 4, :, :] = result(s, u, coef, half, row, c, total)
@@ -427,11 +431,11 @@
     right, left, to_near, to_far, tiny_near, tiny_far, te, ts, tx = call(
         pack_kernel,
         [HBM] * 6,
-        [pltpu.VMEM((MAIN_MSG, 128), F32)] * 4 + [pltpu.VMEM((TINY_MSG, 128), F32)] * 2 + [TURNED] * 3,
+        [pltpu.VMEM((MAIN_MSG, 128), F32)] * 2 + [pltpu.VMEM((5, SIDE, 256), F32)] * 2 + [pltpu.VMEM((TINY_MSG, 128), F32)] * 2 + [TURNED] * 3,
         [VMEM] * 9,
         [pltpu.SMEM((8,), F32)]
         + [pltpu.VMEM((SIDE, SIDE), kind) for kind in (jnp.int32, jnp.int32, F32, jnp.int32)]
-        + [pltpu.VMEM((2, 2, SIDE, 8, 128), F32), DMA((2, 2)), DMA((2, 2, 4)), DMA((5,))],
+        + [pltpu.VMEM((2, SIDE, 8, 256), F32), DMA((2,)), DMA((2,)), DMA((5,))],
         1 << 22,
         4,
     )(*given)
@@ -451,32 +455,32 @@
         [VMEM] * 10,
         [FIELD, FIELD, COEF, FIELD, FIELD, pltpu.VMEM((2, SIDE, SIDE, 128), F32)],
         [VMEM] * 6,
-        [FACTORS],
+        [TURNED] * 3 + [FACTORS],
         1 << 25,
         4,
         {7 + i: i for i in range(3)},
-    )(te2, ts2, tx2, one, other, to_near, to_far, s, x1, coef)
+    )(te, ts, tx, one, other, to_near, to_far, s, x1, coef)
     strip = pltpu.VMEM((2, SIDE, 8, 128), F32)
     *state, out, left_strip = call(
         functools.partial(side_kernel, 0),
         [VMEM] * 13,
         [FIELD, FIELD, COEF, FIELD, FIELD, potential, strip],
         [VMEM] * 5 + [HBM, VMEM],
-        [TURNED] * 3 + [FACTORS, DMA((5, 2))],
+        [TURNED] * 3 + [FACTORS, DMA((5, 3))],
         1 << 23,
         4,
         {8 + i: i for i in range(5)},
     )(te2, ts2, tx2, from_left, left, one, other, middle, *state)
     *state, out = call(
         functools.partial(side_kernel, 1),
-        [VMEM] * 10 + [HBM],
+        [VMEM] * 11 + [HBM],
         [FIELD, FIELD, COEF, FIELD, FIELD, potential],
         [VMEM] * 5 + [HBM],
-        [strip] + [TURNED] * 3 + [FACTORS, DMA((5, 2))],
+        [strip] + [TURNED] * 3 + [FACTORS, DMA((5, 3))],
         1 << 23,
         4,
-        {5 + i: i for i in range(6)},
-    )(te2, ts2, tx2, from_right, left_strip, *state, out)
+        {6 + i: i for i in range(6)},
+    )(te2, ts2, tx2, from_right, middle, left_strip, *state, out)
     return out
 
 

time: 35.9 us -> 32.5 us (0.905)
  waiting for transfers between devices: 8.77 us -> 4.98 us
  starting transfers between devices: 10.9 us -> 13 us
  Pallas kernels: 16.1 us -> 14.4 us
    ppermute x2, waiting for transfers between devices: 8.76 us -> 4.97 us  [exchange(): lax.ppermute(far, 'gx', [(i, (i - 1 + 2 * (i % 2)) % count) for i in rang...]
    ppermute x2, starting transfers between devices: 1.77 us -> 3.86 us  [exchange(): lax.ppermute(far, 'gx', [(i, (i - 1 + 2 * (i % 2)) % count) for i in rang...]
    pallas_call x2, Pallas kernels: 4.79 us -> 3.77 us  [the longest x1 2.13 us: block(): call(functools.partial(side_kernel, 1), [VMEM] * 11 + [HBM], [FIELD, FIEL...]
    pallas_call x1, Pallas kernels: 2.22 us -> 1.5 us  [block(): call(functools.partial(side_kernel, 0), [VMEM] * 13, [FIELD, FIELD, COEF,...]
  transfers between devices with their start and end apart: 6 -> 6, of which waited for: 2 -> 1; matrix products, arithmetic and copies ran while one was open for 0% -> 0% of each run, Pallas kernels for 31% -> 33%
where the time goes in v6:
time: 32.5 us; the launch traced here: 32.4 us
  Pallas kernels  14.4 us (44%)
  starting transfers between devices  13 us (40%)
  waiting for transfers between devices  4.98 us (15%)
    ppermute x2, starting transfers between devices, shift(): lax.ppermute(values, 'gy', [(i, (i + step) % count) for i in range(count)])  8.36 us
    pallas_call x1, Pallas kernels, block(): call(main_kernel, [VMEM] * 10, [FIELD, FIELD, COEF, FIELD, FIELD, pltpu.V...  5.72 us
    ppermute x2, waiting for transfers between devices, exchange(): lax.ppermute(far, 'gx', [(i, (i - 1 + 2 * (i % 2)) % count) for i in rang...  4.97 us
    ppermute x2, starting transfers between devices, exchange(): lax.ppermute(far, 'gx', [(i, (i - 1 + 2 * (i % 2)) % count) for i in rang...  3.86 us
    pallas_call x1, Pallas kernels, block(): call(first_kernel, [VMEM] * 4, [FIELD, FIELD, COEF], [VMEM] * 3, [FACTORS...  3.27 us
    pallas_call x1, Pallas kernels, block(): call(functools.partial(side_kernel, 1), [VMEM] * 11 + [HBM], [FIELD, FIEL...  2.13 us
    pallas_call x1, Pallas kernels, block(): call(pack_kernel, [HBM] * 6, [pltpu.VMEM((MAIN_MSG, 128), F32)] * 2 + [pl...  1.64 us
    pallas_call x1, Pallas kernels, block(): call(functools.partial(side_kernel, 0), [VMEM] * 13, [FIELD, FIELD, COEF,...  1.5 us
  transfers between devices with their start and end apart: 6, of which 1 were waited for; matrix products, arithmetic and copies ran while one was open for 0% of the time, Pallas kernels for 33%

profile of v6, /device:TPU:7, one launch (start us, length us, event | category | flops | bytes accessed | tf_op | source)
XLA Modules:
  0.0 32.4 jit_solution(8718041429881340063)
XLA Ops:
  0.0 0.0 copy-start
  0.0 1.6 %shard_map.64 = (f32[512,128]{1,0:T(8,128)S(1)}, f32[512,128]{1,0:T(8,128)S(1)}, f32[5,64,256]{2,1,0:T(8,128)S(1)}, f32[5,64,256]{2,1,0:T(8,128)S(1)}, f32[40,12...) custom-call(f32[8]{0:T(128)} %refs_0_.1, ...), custom_call_target="tpu_custom_call" | custom-call | flops 4194304 | bytes 1048576 | tf_op jit(solution)/shard_map/pallas_call | solution.py:431
  1.7 0.8 %collective-permute-start.3 = (f32[5,64,256]{2,1,0:T(8,128)S(1)}, f32[5,64,256]{2,1,0:T(8,128)S(1)}, u32[]{:S(2)}, u32[]{:S(2)}) collective-permute-start(f32[5,64,256]{2,1,0:T(8,128)S(1)} %get-tuple-element.48.own_near), channel_id=1, source_target_pairs={{0,16},{16,0},{32,48},{48,32},{64,80},{80,64},{96,112},{112,96},{1... | collective-permute-start | bytes 983048 | tf_op jit(solution)/shard_map/ppermute | solution.py:420
  2.4 1.2 %collective-permute-start.4 = (f32[5,64,256]{2,1,0:T(8,128)S(1)}, f32[5,64,256]{2,1,0:T(8,128)S(1)}, u32[]{:S(2)}, u32[]{:S(2)}) collective-permute-start(f32[5,64,256]{2,1,0:T(8,128)S(1)} %get-tuple-element.49.own_far), channel_id=1, source_target_pairs={{0,240},{16,32},{32,16},{48,64},{64,48},{80,96},{96,80},{112,128},... | collective-permute-start | bytes 983048 | tf_op jit(solution)/shard_map/ppermute | solution.py:419
  3.6 0.0 collective-permute-start
  3.6 2.7 %collective-permute-start.1 = (f32[40,128]{1,0:T(8,128)S(1)}, f32[40,128]{1,0:T(8,128)S(1)}, u32[]{:S(2)}, u32[]{:S(2)}) collective-permute-start(f32[40,128]{1,0:T(8,128)S(1)} %get-tuple-element.41), channel_id=1, source_target_pairs={{0,240},{16,32},{32,16},{48,64},{64,48},{80,96},{96,80},{112,128},... | collective-permute-start | bytes 61448 | tf_op jit(solution)/shard_map/ppermute | solution.py:419
  6.3 0.0 collective-permute-done.near
  6.3 5.0 %collective-permute-done.1.far = f32[40,128]{1,0:T(8,128)S(1)} collective-permute-done((f32[40,128]{1,0:T(8,128)S(1)}, f32[40,128]{1,0:T(8,128)S(1)}, u32[]{:S(2)}, u32[]{:S(2)}) %collective-permute-start.1) | collective-permute-done | bytes 20512 | tf_op jit(solution)/shard_map/ppermute | solution.py:419
  11.2 0.1 shard_map.65
  11.4 3.0 %collective-permute-start.5 = (f32[552,128]{1,0:T(8,128)S(1)}, f32[552,128]{1,0:T(8,128)S(1)}, u32[]{:S(2)}, u32[]{:S(2)}) collective-permute-start(f32[552,128]{1,0:T(8,128)S(1)} %get-tuple-element.55), channel_id=1, source_target_pairs={{0,1},{1,2},{2,3},{3,4},{4,5},{5,6},{6,7},{7,8},{8,9},{9,10},{10,1... | collective-permute-start | bytes 847880 | tf_op jit(solution)/shard_map/ppermute | solution.py:427
  14.4 5.4 %collective-permute-start.2 = (f32[552,128]{1,0:T(8,128)S(1)}, f32[552,128]{1,0:T(8,128)S(1)}, u32[]{:S(2)}, u32[]{:S(2)}) collective-permute-start(f32[552,128]{1,0:T(8,128)S(1)} %get-tuple-element.47), channel_id=1, source_target_pairs={{0,15},{1,0},{2,1},{3,2},{4,3},{5,4},{6,5},{7,6},{8,7},{9,8},{10,9... | collective-permute-start | bytes 847880 | tf_op jit(solution)/shard_map/ppermute | solution.py:427
  19.7 0.0 copy-done
  19.7 3.3 %shard_map.66 = (f32[2,72,80,128]{3,2,1,0:T(8,128)S(1)}, f32[2,72,80,128]{3,2,1,0:T(8,128)S(1)}, f32[3,72,80,128]{3,2,1,0:T(8,128)S(1)}) custom-call(f32[88,128]{1,0:T(8,128)S(1)} %get-tuple-element.37.te.own_te, f32[88,128]{1,0:T(8,128)S(1)} %get-tuple-element.38.ts.own_ts, f32[88,128]{1,0:T(8,128)S(1)} %get-tuple-element.39.tx.own_tx, ...), custom_call_target="tpu_custom_call" | custom-call | flops 33554432 | bytes 1048576 | tf_op jit(solution)/shard_map/pallas_call | solution.py:450
  23.0 0.0 collective-permute-done.3.near.refs_5_
  23.0 0.0 collective-permute-done.4.far.refs_6_
  23.0 5.7 %shard_map.67 = (f32[2,72,80,128]{3,2,1,0:T(8,128)S(1)}, f32[2,72,80,128]{3,2,1,0:T(8,128)S(1)}, f32[3,72,80,128]{3,2,1,0:T(8,128)S(1)}, f32[2,72,80,128]{3,2,1,...) custom-call(f32[88,128]{1,0:T(8,128)S(1)} %get-tuple-element.37.te.o, ...), custom_call_target="tpu_custom_call", output_to_operand_aliasing={{0}: (7, {}), {1}: (8, {}), {2}: (9, {})} | custom-call | flops 33554432 | bytes 1048576 | tf_op jit(solution)/shard_map/pallas_call | solution.py:453
  28.8 0.0 collective-permute-done.5.refs_3_
  28.8 1.5 %shard_map.68 = (f32[2,72,80,128]{3,2,1,0:T(8,128)S(1)}, f32[2,72,80,128]{3,2,1,0:T(8,128)S(1)}, f32[3,72,80,128]{3,2,1,0:T(8,128)S(1)}, f32[2,72,80,128]{3,2,1,...) custom-call(f32[88,128]{1,0:T(8,128)S(1)} %get-tuple-element.44.refs, ...), custom_call_target="tpu_custom_call", output_to_operand_aliasing={{0}: (8, {}), {1}: (9, {}), {2}: (10, {}), {3}: (11, {}), {... | custom-call | flops 8388608 | bytes 1048576 | tf_op jit(solution)/shard_map/pallas_call | solution.py:464
  30.3 0.0 collective-permute-done.2.refs_3_
  30.3 2.1 %shard_map.69 = (f32[2,72,80,128]{3,2,1,0:T(8,128)S(1)}, f32[2,72,80,128]{3,2,1,0:T(8,128)S(1)}, f32[3,72,80,128]{3,2,1,0:T(8,128)S(1)}, f32[2,72,80,128]{3,2,1,...) custom-call(f32[88,128]{1,0:T(8,128)S(1)} %get-tuple-element.44.refs, ...), custom_call_target="tpu_custom_call", output_to_operand_aliasing={{0}: (6, {}), {1}: (7, {}), {2}: (8, {}), {3}: (9, {}), {4}... | custom-call | flops 8388608 | bytes 1048576 | tf_op jit(solution)/shard_map/pallas_call | solution.py:474
Async XLA Ops:
  0.0 19.7 %copy-start = (f32[64,64,256]{2,1,0:T(8,128)S(1)}, f32[64,64,256]{2,1,0:T(8,128)}, u32[]{:S(2)}) copy-start(f32[64,64,256]{2,1,0:T(8,128)} %load) | copy-start | bytes 12582916
  1.7 21.4 %collective-permute-start.3 = (f32[5,64,256]{2,1,0:T(8,128)S(1)}, f32[5,64,256]{2,1,0:T(8,128)S(1)}, u32[]{:S(2)}, u32[]{:S(2)}) collective-permute-start(f32[5,64,256]{2,1,0:T(8,128)S(1)} %get-tuple-element.48.own_near), channel_id=1, source_target_pairs={{0,16},{16,0},{32,48},{48,32},{64,80},{80,64},{96,112},{112,96},{1... | collective-permute-start | bytes 983048 | tf_op jit(solution)/shard_map/ppermute | solution.py:420
  2.4 20.6 %collective-permute-start.4 = (f32[5,64,256]{2,1,0:T(8,128)S(1)}, f32[5,64,256]{2,1,0:T(8,128)S(1)}, u32[]{:S(2)}, u32[]{:S(2)}) collective-permute-start(f32[5,64,256]{2,1,0:T(8,128)S(1)} %get-tuple-element.49.own_far), channel_id=1, source_target_pairs={{0,240},{16,32},{32,16},{48,64},{64,48},{80,96},{96,80},{112,128},... | collective-permute-start | bytes 983048 | tf_op jit(solution)/shard_map/ppermute | solution.py:419
  3.6 2.7 %collective-permute-start = (f32[40,128]{1,0:T(8,128)S(1)}, f32[40,128]{1,0:T(8,128)S(1)}, u32[]{:S(2)}, u32[]{:S(2)}) collective-permute-start(f32[40,128]{1,0:T(8,128)S(1)} %get-tuple-element.40), channel_id=1, source_target_pairs={{0,16},{16,0},{32,48},{48,32},{64,80},{80,64},{96,112},{112,96},{1... | collective-permute-start | bytes 61448 | tf_op jit(solution)/shard_map/ppermute | solution.py:420
  3.6 7.6 %collective-permute-start.1 = (f32[40,128]{1,0:T(8,128)S(1)}, f32[40,128]{1,0:T(8,128)S(1)}, u32[]{:S(2)}, u32[]{:S(2)}) collective-permute-start(f32[40,128]{1,0:T(8,128)S(1)} %get-tuple-element.41), channel_id=1, source_target_pairs={{0,240},{16,32},{32,16},{48,64},{64,48},{80,96},{96,80},{112,128},... | collective-permute-start | bytes 61448 | tf_op jit(solution)/shard_map/ppermute | solution.py:419
  11.4 17.4 %collective-permute-start.5 = (f32[552,128]{1,0:T(8,128)S(1)}, f32[552,128]{1,0:T(8,128)S(1)}, u32[]{:S(2)}, u32[]{:S(2)}) collective-permute-start(f32[552,128]{1,0:T(8,128)S(1)} %get-tuple-element.55), channel_id=1, source_target_pairs={{0,1},{1,2},{2,3},{3,4},{4,5},{5,6},{6,7},{7,8},{8,9},{9,10},{10,1... | collective-permute-start | bytes 847880 | tf_op jit(solution)/shard_map/ppermute | solution.py:427
  14.4 15.9 %collective-permute-start.2 = (f32[552,128]{1,0:T(8,128)S(1)}, f32[552,128]{1,0:T(8,128)S(1)}, u32[]{:S(2)}, u32[]{:S(2)}) collective-permute-start(f32[552,128]{1,0:T(8,128)S(1)} %get-tuple-element.47), channel_id=1, source_target_pairs={{0,15},{1,0},{2,1},{3,2},{4,3},{5,4},{6,5},{7,6},{8,7},{9,8},{10,9... | collective-permute-start | bytes 847880 | tf_op jit(solution)/shard_map/ppermute | solution.py:427
